TPU v7x, 128 devices: a 2x2x16 block of a 8x8x16 slice. The times are simulated.
128 devices in a mesh: group: 4 (over y, x), ep: 32 (over z, core).
Axes of the slice: x: 2, y: 2, z: 16, core: 2. Of those that a mesh axis runs over, the one named last changes fastest.
The devices are a block of a 8x8x16 slice.
Arguments:
- tokens: bfloat16 [8192, 3072], P(('group', 'ep')), parts along dimension 0, may hold values from -6 to 6
- expert_ids: int32 [8192, 2], P(('group', 'ep')), parts along dimension 0, may hold values from 0 to 3, all different within a row; in each aligned block of 64 rows (0 to 63, 64 to 127, ...) at most 48 rows name the same one
- w_router: bfloat16 [3072, 4], replicated, may hold values from -0.109375 to 0.109375
- w_gate: bfloat16 [3072, 32768], P(None, 'ep'), may hold values from -0.109375 to 0.109375
- w_up: bfloat16 [3072, 32768], P(None, 'ep'), may hold values from -0.109375 to 0.109375
- w_down: bfloat16 [32768, 3072], P('ep'), may hold values from -0.0625 to 0.0625
- queries: bfloat16 [1024, 24, 128], P(('group', 'ep')), parts along dimension 0, may hold values from -48 to 48
- key_cache: bfloat16 [1024, 256, 4, 128], P(('group', 'ep')), parts along dimension 0, may hold values from -48 to 48
- cached_value_rows: bfloat16 [1024, 256, 4, 128], P(('group', 'ep')), parts along dimension 0, may hold values from -6 to 6
- lengths: int32 [1024], P(('group', 'ep')), parts along dimension 0, may hold values from 2 to 256, as said below
Outputs:
- moe_out: bfloat16 [8192, 3072], P(('group', 'ep')), parts along dimension 0
- attention_out: bfloat16 [1024, 24, 128], P(('group', 'ep')), parts along dimension 0
There are 4 independent parts, one for each index of `group`. A program takes and returns all parts, laid end to end along the dimension named above; an argument that names none is the same for every part. Nothing has to cross between parts.
Inputs may be any that keep to these rules, and one draw needn't show every extreme that they name: `expert_ids`: each row names two different experts; among the rows of one device no expert is named more than 48 times, and some device has an expert named exactly 48 times. `lengths`: every device holds a request of length 256.
All inputs are finite; a program needn't handle non-finite values.
Results may differ from a plain program's by a relative error of at most 0.0085.
Values may be sent and summed in bfloat16 or wider, within the bound.
No kernel may reach another device: no remote copies, remote signals or barrier semaphores. Data moves between devices by JAX's collectives and lax.ppermute only.
A program may use at most 128 MiB of HBM per device.

v0:
```python
import jax
import jax.numpy as jnp
from jax import lax
from jax.sharding import PartitionSpec as P

CAP = 48


def sent_together(arrays, axis, dim, along):
    ends, at = ([], 0)
    for a in arrays[:-1]:
        at += a.shape[along]
        ends.append(at)
    both = jnp.concatenate(arrays, axis=along)
    return tuple(jnp.split(lax.all_gather(both, axis, axis=dim, tiled=True), ends, axis=along))


def expert_mlp(inputs, gate_part, up_part, down_part):
    gate_value = jnp.dot(inputs, gate_part, preferred_element_type=jnp.float32)
    up_value = jnp.dot(inputs, up_part, preferred_element_type=jnp.float32)
    hidden = (jax.nn.silu(gate_value) * up_value).astype(jnp.bfloat16)
    return jnp.dot(hidden, down_part, preferred_element_type=jnp.float32).astype(jnp.bfloat16)


def route_tables(tokens, expert_ids, w_router, capacity):
    token_count = tokens.shape[0]
    expert_count = w_router.shape[1]
    logits = jnp.dot(tokens, w_router, preferred_element_type=jnp.float32)
    labels = jnp.arange(expert_count, dtype=jnp.int32)
    onehot = expert_ids[:, :, None] == labels[None, None, :]
    picked = jnp.sum(jnp.where(onehot, logits[:, None, :], jnp.float32(0.0)), axis=2)
    gate_values = 1.0 / (1.0 + jnp.exp(picked[:, ::-1] - picked))
    flat_hits = onehot.reshape(token_count * 2, expert_count).astype(jnp.int32)
    earlier = jnp.cumsum(flat_hits, axis=0) - flat_hits
    position = jnp.sum(earlier * flat_hits, axis=1).reshape(token_count, 2)
    return (gate_values, expert_ids * capacity + position)


def decode_attention(queries, key_cache, cached_value_rows, lengths):
    request_count, head_count, head_dim = queries.shape
    cache_len = key_cache.shape[1]
    kv_heads = key_cache.shape[2]
    grouped = queries.reshape(request_count, kv_heads, head_count // kv_heads, head_dim)
    scores = jnp.einsum(
        "bkgd,blkd->bkgl", grouped, key_cache, preferred_element_type=jnp.float32
    ) * head_dim ** (-0.5)
    visible = jnp.arange(cache_len, dtype=jnp.int32)[None, :] < lengths[:, None]
    scores = jnp.where(visible[:, None, None, :], scores, -jnp.inf)
    row_max = jnp.max(scores, axis=3, keepdims=True)
    exponent = jnp.exp(scores - row_max)
    weights = (exponent / jnp.sum(exponent, axis=3, keepdims=True)).astype(jnp.bfloat16)
    mixed = jnp.einsum(
        "bkgl,blkd->bkgd", weights, cached_value_rows, preferred_element_type=jnp.float32
    )
    return mixed.reshape(request_count, head_count, head_dim).astype(jnp.bfloat16)


def on_device(
    tokens,
    expert_ids,
    w_router,
    w_gate,
    w_up,
    w_down,
    queries,
    key_cache,
    cached_value_rows,
    lengths,
):
    attention_out = decode_attention(queries, key_cache, cached_value_rows, lengths)
    expert_count = w_router.shape[1]
    token_count = tokens.shape[0]
    feature_width = tokens.shape[1]
    shard_count = lax.axis_size("ep")
    tp_width = shard_count // expert_count
    gathered, gathered_ids = sent_together((tokens, expert_ids.astype(jnp.bfloat16)), "ep", 0, 1)
    source_tokens = gathered.reshape(shard_count, token_count, feature_width)
    source_ids = gathered_ids.astype(jnp.int32).reshape(shard_count, token_count, 2)

    def per_source(block_tokens, block_choice):
        return route_tables(block_tokens, block_choice, w_router, CAP)

    gate_values, slot_index = jax.vmap(per_source)(source_tokens, source_ids)
    own_expert = lax.axis_index("ep") // tp_width
    local_slot = slot_index - own_expert * CAP
    slot_labels = jnp.arange(CAP, dtype=jnp.int32)
    matches = local_slot[:, None, :, :] == slot_labels[None, :, None, None]
    selector = jnp.any(matches, axis=3).astype(jnp.bfloat16)
    packed = jnp.einsum(
        "sct,std->scd", selector, source_tokens, preferred_element_type=jnp.float32
    ).astype(jnp.bfloat16)
    partial_value = expert_mlp(
        packed.reshape(shard_count * CAP, feature_width), w_gate, w_up, w_down
    )
    partial_value = lax.optimization_barrier(partial_value)
    partial_value = partial_value.astype(jnp.float32).reshape(shard_count, CAP, feature_width)
    weight_table = jnp.sum(jnp.where(matches, gate_values[:, None, :, :], jnp.float32(0.0)), axis=3)
    terms = jnp.einsum(
        "sct,scd->std", weight_table, partial_value, preferred_element_type=jnp.float32
    )
    moe_out = lax.psum_scatter(
        terms.reshape(token_count * lax.axis_size("ep"), feature_width),
        "ep",
        scatter_dimension=0,
        tiled=True,
    ).astype(jnp.bfloat16)
    return (moe_out, attention_out)


def solution(mesh):
    in_specs = (
        P(("group", "ep"), None),
        P(("group", "ep"), None),
        P(),
        P(None, "ep"),
        P(None, "ep"),
        P("ep", None),
        P(("group", "ep"), None, None),
        P(("group", "ep"), None, None, None),
        P(("group", "ep"), None, None, None),
        P(("group", "ep")),
    )
    out_specs = (P(("group", "ep"), None), P(("group", "ep"), None, None))
    return jax.shard_map(
        on_device, mesh=mesh, in_specs=in_specs, out_specs=out_specs, check_vma=False
    )
```

profile of v0, /device:TPU:70, one launch (start us, length us, event | category | flops | bytes accessed | tf_op | source)
XLA Modules:
  0.0 343.9 jit_solution(6114936067617400986)
XLA Ops:
  7.2 0.0 copy-start
  7.2 0.1 all-gather.2.cloned.1.call-start
  7.3 0.8 convert_element_type.32
  8.1 0.1 copy.41
  8.2 1.8 pad_maximum_fusion
  10.0 0.1 all-gather.2.cloned.1.call-update
  10.1 0.1 reduce-scatter.2.cloned.1.call-start
  10.2 0.0 copy-start.3
  10.2 91.0 %all-gather.2.cloned.1.call-done = bf16[2048,3074]{1,0:T(8,128)(2,1)} async-done(((bf16[64,3074]{1,0:T(8,128)(2,1)}), bf16[2048,3074]{1,0:T(8,128)(2,1)}) %all-gather.2.cloned.1.call-update) | async-done | bytes 12591120 | tf_op jit(solution)/shard_map/all_gather | solution.py:15
  101.2 6.2 %split.9 = bf16[2048,3072]{1,0:T(8,128)(2,1)S(1)} slice(bf16[2048,3074]{1,0:T(8,128)(2,1)} %all-gather.2.cloned.1.call-done), slice={[0:2048], [0:3072]} | slice | bytes 25165824 | tf_op jit(solution)/shard_map/split | solution.py:15
  107.4 5.0 %fusion.28 = f32[32,64,4]{1,2,0:T(4,128)S(1)} fusion(bf16[32,64,3072]{2,1,0:T(8,128)(2,1)S(1)} %bitcast.23, bf16[3072,4]{0,1:T(4,128)(2,1)S(1)} %copy-done.3), kind=kOutput, calls=%fused_computation.36 | convolution fusion | flops 50331648 | bytes 12640256 | tf_op jit(solution)/shard_map/vmap()/dot_general | solution.py:28
  112.4 1.1 slice_convert_fusion
  113.6 0.5 eq.35
  114.0 0.4 copy.54
  114.5 0.1 copy.43
  114.6 3.3 fusion.5
  117.9 0.1 copy.44
  118.1 0.3 fusion.10
  118.4 0.4 select_reduce_fusion
  118.8 10.8 %convolution_convert_fusion.1 = bf16[32,48,3072]{2,1,0:T(8,128)(2,1)} fusion(pred[32,48,64]{2,1,0:T(8,128)(4,1)S(1)} %fusion.10, bf16[32,64,3072]{2,1,0:T(8,128)(2,1)} %bitcast.24), kind=kOutput, calls=%fused_computation.2 | convolution fusion | flops 608698368 | bytes 22118400 | tf_op jit(solution)/shard_map/sct,std->scd/dot_general | solution.py:89
  129.5 15.3 %fusion.32 = f32[1536,1024]{1,0:T(8,128)} fusion(bf16[1536,3072]{1,0:T(8,128)(2,1)} %bitcast.26, bf16[3072,1024]{1,0:T(8,128)(2,1)} %param.13), kind=kOutput, calls=%fused_computation.41 | convolution fusion | flops 9663676416 | bytes 22020096 | tf_op jit(solution)/shard_map/dot_general | solution.py:19
  144.8 28.0 %convolution_convert_fusion = bf16[1536,3072]{1,0:T(8,128)(2,1)} fusion(bf16[1024,3072]{1,0:T(8,128)(2,1)} %param.15, f32[1536,1024]{1,0:T(8,128)} %fusion.32, bf16[1536,3072]{1,0:T(8,128)(2,1)} %bitcast.27, bf16[3072,1024]{1,0:T(8,128)(2,1)} %param.14), kind=kOutput, calls=%fused_computation.1 | convolution fusion | flops 19341508608 | bytes 37748736 | tf_op jit(solution)/shard_map/dot_general | solution.py:22
  172.9 15.4 %fusion.33 = f32[32,64,3072]{2,1,0:T(8,128)} fusion(bf16[32,48,64]{2,1,0:T(8,128)(2,1)S(1)} %select_reduce_fusion, bf16[32,48,3072]{2,1,0:T(8,128)(2,1)} %bitcast.28), kind=kOutput, calls=%fused_computation.42 | convolution fusion | flops 603979776 | bytes 34799616 | tf_op jit(solution)/shard_map/sct,scd->std/dot_general | solution.py:98
  188.3 0.1 reduce-scatter.2.cloned.1.call-update
  188.4 0.7 copy-done.2
  189.1 0.1 iota_compare_fusion.4
  189.2 0.6 fusion.15
  189.8 0.2 fusion.31
  190.1 2.2 fusion.19
  192.3 0.6 copy.53
  192.9 142.3 %reduce-scatter.2.cloned.1.call-done = f32[64,3072]{1,0:T(8,128)} async-done(((f32[2048,3072]{1,0:T(8,128)}), f32[64,3072]{1,0:T(8,128)}) %reduce-scatter.2.cloned.1.call-update) | async-done | bytes 786448 | tf_op jit(solution)/shard_map/reduce_scatter | solution.py:101
  335.2 1.9 convert_element_type.38
  (15 shorter events, 0.2 us)
Async XLA Ops:
  7.2 182.0 %copy-start = (bf16[8,256,4,128]{3,2,1,0:T(4,128)(2,1)S(1)}, bf16[8,256,4,128]{3,2,1,0:T(4,128)(2,1)}, u32[]{:S(2)}) copy-start(bf16[8,256,4,128]{3,2,1,0:T(4,128)(2,1)} %param.17) | copy-start | bytes 6291460
  7.2 94.0 %all-gather.2.cloned.1.call-start = ((), (), s32[]{:S(2)}) async-start(), calls=%async_computation.1 | async-start | bytes 13516800 | tf_op jit(solution)/shard_map/all_gather | solution.py:15
  10.1 325.1 %reduce-scatter.2.cloned.1.call-start = ((), (), s32[]{:S(2)}) async-start(), calls=%async_computation.2 | async-start | bytes 25952256 | tf_op jit(solution)/shard_map/reduce_scatter | solution.py:101
  10.2 97.3 %copy-start.3 = (bf16[3072,4]{0,1:T(4,128)(2,1)S(1)}, bf16[3072,4]{0,1:T(4,128)(2,1)}, u32[]{:S(2)}) copy-start(bf16[3072,4]{0,1:T(4,128)(2,1)} %param.12) | copy-start | bytes 73732
  107.4 5.0 %copy-start.1 = (bf16[2048,3072]{1,0:T(8,128)(2,1)}, bf16[2048,3072]{1,0:T(8,128)(2,1)S(1)}, u32[]{:S(2)}) copy-start(bf16[2048,3072]{1,0:T(8,128)(2,1)S(1)} %split.9) | copy-start | bytes 37748740
  188.3 0.8 copy-start.2
  188.3 0.8 copy-start.4
Sparse Core Ops, SparseCore 0:
  10.2 90.9 all-gather.1
  188.5 146.6 reduce-scatter.1
where the time goes:
time: 344 us
  waiting for transfers between devices  233 us (68%)
  matrix products  77.3 us (22%)
  between operations  14.2 us (4%)
  other arithmetic  10.1 us (3%)
  local copies, waits for them, and re-layouts  8.86 us (3%)
    reduce_scatter x1, waiting for transfers between devices, on_device(): lax.psum_scatter(terms.reshape(token_count * lax.axis_size('ep'), feature...  142 us
    all_gather x1, waiting for transfers between devices, sent_together(): lax.all_gather(both, axis, axis=dim, tiled=True)  91 us
    dot_general x1, matrix products, expert_mlp(): jnp.dot(hidden, down_part, preferred_element_type=jnp.float32)  28 us
    dot_general x1, matrix products, on_device(): jnp.einsum('sct,scd->std', weight_table, partial_value, preferred_element...  15.4 us
    dot_general x1, matrix products, expert_mlp(): gate_value = jnp.dot(inputs, gate_part, preferred_element_type=jnp.float32)  15.3 us
    dot_general x1, matrix products, on_device(): jnp.einsum('sct,std->scd', selector, source_tokens, preferred_element_typ...  10.8 us
  transfers between devices with their start and end apart: 2, of which 2 were waited for; matrix products, arithmetic and copies ran while one was open for 1% of the time, Pallas kernels for 0%

commit v1 on v0

v1 whole, which is shorter than its diff:
```python
import functools

import jax
import jax.numpy as jnp
from jax import lax
from jax.experimental import pallas as pl
from jax.experimental.pallas import tpu as pltpu
from jax.sharding import PartitionSpec as P


PAD = 128
VMEM_LIMIT = 8 * 2**20
LOAD_LIMIT = 30 * 2**20
AHEAD = 2


def store_rows(outs, y, gate, cols, segments):
    for index, to, start, count in segments:
        rows = y[start:start + count] * gate[start:start + count]
        outs[index][to:to + count, cols] = rows.astype(jnp.bfloat16)


def row_gates(xs, sel, d):
    return jnp.concatenate([
        jnp.sum(x_ref[:, d:].astype(jnp.float32) * sel[0:1, :], axis=1, keepdims=True)
        for x_ref in xs
    ], axis=0)


def mlp_body(n, outs, segments, up_parts, down_parts, *refs):
    xs = refs[:n]
    sel, wg, wu, wd = refs[n:n + 4]
    ys = refs[n + 4:n + 4 + outs]
    hbuf = refs[n + 4 + outs]
    d, ff = wg.shape
    bh, by = ff // up_parts, d // down_parts

    def up_step(j, carry):
        cols = pl.ds(pl.multiple_of(j * bh, bh), bh)
        x = jnp.concatenate([x_ref[:, :d] for x_ref in xs], axis=0)
        g = jnp.dot(x, wg[:, cols], preferred_element_type=jnp.float32)
        u = jnp.dot(x, wu[:, cols], preferred_element_type=jnp.float32)
        hbuf[:, cols] = (g / (1.0 + jnp.exp(-g)) * u).astype(jnp.bfloat16)
        return carry

    lax.fori_loop(0, up_parts, up_step, 0)
    gate = row_gates(xs, sel, d)

    def down_step(j, carry):
        cols = pl.ds(pl.multiple_of(j * by, by), by)
        y = jnp.dot(hbuf[...], wd[:, cols], preferred_element_type=jnp.float32)
        store_rows(ys, y, gate, cols, segments)
        return carry

    lax.fori_loop(0, down_parts, down_step, 0)


def mlp(xs, sel, wg, wu, wd, out_rows, segments, up_parts=4, down_parts=6):
    d, ff = wg.shape
    n, total = len(xs), sum(x.shape[0] for x in xs)
    vmem = pl.BlockSpec(memory_space=pltpu.VMEM)
    return pl.pallas_call(
        functools.partial(mlp_body, n, len(out_rows), segments, up_parts, down_parts),
        in_specs=[vmem] * (n + 4),
        out_specs=[vmem] * len(out_rows),
        out_shape=[jax.ShapeDtypeStruct((r, d), jnp.bfloat16) for r in out_rows],
        scratch_shapes=[pltpu.VMEM((total, ff), jnp.bfloat16)],
        compiler_params=pltpu.CompilerParams(vmem_limit_bytes=VMEM_LIMIT),
        cost_estimate=pl.CostEstimate(
            flops=6 * total * d * ff, bytes_accessed=6 * d * ff, transcendentals=total * ff
        ),
        name="mlp",
    )(*xs, sel, wg, wu, wd)


def load_body(n, rows, parts, *refs):
    xs = refs[:n]
    sel, wg, wu, wd = refs[n:n + 4]
    ys = refs[n + 4:2 * n + 4]
    gv, uv, dv, hbuf, sg, su, sd = refs[2 * n + 4:]
    d, ff = wg.shape
    bh, by = ff // parts, d // parts
    offs = [sum(rows[:i]) for i in range(n)]

    def up_copies(j):
        cols = pl.ds(pl.multiple_of(j * bh, bh), bh)
        return (
            pltpu.make_async_copy(wg.at[:, cols], gv.at[:, cols], sg.at[j]),
            pltpu.make_async_copy(wu.at[:, cols], uv.at[:, cols], su.at[j]),
        )

    def down_copy(j):
        cols = pl.ds(pl.multiple_of(j * by, by), by)
        return pltpu.make_async_copy(wd.at[:, cols], dv.at[:, cols], sd.at[j])

    def start_up(j):
        for c in up_copies(j):
            c.start()

    for j in range(AHEAD):
        start_up(j)

    def up_step(j, carry):
        for c in up_copies(j):
            c.wait()
        pl.when(j < parts - AHEAD)(lambda: start_up(j + AHEAD))
        pl.when(j >= parts - AHEAD)(lambda: down_copy(j - (parts - AHEAD)).start())
        cols = pl.ds(pl.multiple_of(j * bh, bh), bh)
        x = jnp.concatenate([x_ref[:, :d] for x_ref in xs], axis=0)
        g = jnp.dot(x, gv[:, cols], preferred_element_type=jnp.float32)
        u = jnp.dot(x, uv[:, cols], preferred_element_type=jnp.float32)
        hbuf[:, cols] = (g / (1.0 + jnp.exp(-g)) * u).astype(jnp.bfloat16)
        return carry

    lax.fori_loop(0, parts, up_step, 0)
    gate = row_gates(xs, sel, d)
    segments = tuple((i, 0, off, r) for i, (off, r) in enumerate(zip(offs, rows)))

    def down_step(j, carry):
        down_copy(j).wait()
        pl.when(j < parts - AHEAD)(lambda: down_copy(j + AHEAD).start())
        cols = pl.ds(pl.multiple_of(j * by, by), by)
        y = jnp.dot(hbuf[...], dv[:, cols], preferred_element_type=jnp.float32)
        store_rows(ys, y, gate, cols, segments)
        return carry

    lax.fori_loop(0, parts, down_step, 0)


def load_and_mlp(xs, sel, wg, wu, wd, parts=4):
    d, ff = wg.shape
    rows = tuple(x.shape[0] for x in xs)
    n, total = len(xs), sum(rows)
    vmem = pl.BlockSpec(memory_space=pltpu.VMEM)
    hbm = pl.BlockSpec(memory_space=pltpu.HBM)
    out = pl.pallas_call(
        functools.partial(load_body, n, rows, parts),
        in_specs=[vmem] * (n + 1) + [hbm] * 3,
        out_specs=[vmem] * (n + 3),
        out_shape=[jax.ShapeDtypeStruct((r, d), jnp.bfloat16) for r in rows]
        + [jax.ShapeDtypeStruct(w.shape, w.dtype) for w in (wg, wu, wd)],
        scratch_shapes=[
            pltpu.VMEM((total, ff), jnp.bfloat16),
            pltpu.SemaphoreType.DMA((parts,)),
            pltpu.SemaphoreType.DMA((parts,)),
            pltpu.SemaphoreType.DMA((parts,)),
        ],
        compiler_params=pltpu.CompilerParams(vmem_limit_bytes=LOAD_LIMIT),
        cost_estimate=pl.CostEstimate(
            flops=6 * total * d * ff, bytes_accessed=6 * d * ff, transcendentals=total * ff
        ),
        name="load_and_mlp",
    )(*xs, sel, wg, wu, wd)
    return out[:n], out[n:]


def gate_table(tokens, expert_ids, w_router):
    expert_count = w_router.shape[1]
    logits = jnp.dot(tokens, w_router, preferred_element_type=jnp.float32)
    labels = jnp.arange(expert_count, dtype=jnp.int32)
    onehot = expert_ids[:, :, None] == labels[None, None, :]
    picked = jnp.sum(jnp.where(onehot, logits[:, None, :], jnp.float32(0.0)), axis=2)
    gate_values = 1.0 / (1.0 + jnp.exp(picked[:, ::-1] - picked))
    return jnp.sum(jnp.where(onehot, gate_values[:, :, None], jnp.float32(0.0)), axis=1)


def decode_attention(queries, key_cache, cached_value_rows, lengths):
    request_count, head_count, head_dim = queries.shape
    cache_len = key_cache.shape[1]
    kv_heads = key_cache.shape[2]
    grouped = queries.reshape(request_count, kv_heads, head_count // kv_heads, head_dim)
    scores = jnp.einsum(
        "bkgd,blkd->bkgl", grouped, key_cache, preferred_element_type=jnp.float32
    ) * head_dim ** (-0.5)
    visible = jnp.arange(cache_len, dtype=jnp.int32)[None, :] < lengths[:, None]
    scores = jnp.where(visible[:, None, None, :], scores, -jnp.inf)
    row_max = jnp.max(scores, axis=3, keepdims=True)
    exponent = jnp.exp(scores - row_max)
    weights = (exponent / jnp.sum(exponent, axis=3, keepdims=True)).astype(jnp.bfloat16)
    mixed = jnp.einsum(
        "bkgl,blkd->bkgd", weights, cached_value_rows, preferred_element_type=jnp.float32
    )
    return mixed.reshape(request_count, head_count, head_dim).astype(jnp.bfloat16)


def total_of(*parts):
    acc = parts[0].astype(jnp.float32)
    for p in parts[1:]:
        acc = acc + p.astype(jnp.float32)
    return acc.astype(jnp.bfloat16)


def on_device(
    tokens,
    expert_ids,
    w_router,
    w_gate,
    w_up,
    w_down,
    queries,
    key_cache,
    cached_value_rows,
    lengths,
):
    experts = w_router.shape[1]
    count, _ = tokens.shape
    shards = lax.axis_size("ep")
    chips = shards // 2
    far = chips // 2
    own_expert = lax.axis_index("ep") // (shards // experts)
    out_ring = [(i, (i + (2 if i % 2 == 0 else -2)) % shards) for i in range(shards)]
    back_ring = [(i, (i - (2 if i % 2 == 0 else -2)) % shards) for i in range(shards)]
    half = count // 2
    pair = [(i, i ^ 1) for i in range(shards)]

    def move(v, pairs):
        return lax.ppermute(v, "ep", pairs)

    table = gate_table(tokens, expert_ids, w_router)
    high = lax.reduce_precision(table, 8, 7)
    extra = jnp.concatenate(
        [high, table - high, jnp.zeros((count, PAD - 2 * experts), jnp.float32)], axis=1
    )
    wide = jnp.concatenate([tokens, extra.astype(jnp.bfloat16)], axis=1)
    lanes = jnp.arange(PAD, dtype=jnp.int32)[None, :]
    picks = (lanes == own_expert) | (lanes == own_expert + experts)
    sel = jnp.broadcast_to(picks.astype(jnp.float32), (8, PAD))

    p_in = q_in = wide
    mine_a, mine_b, sib = {}, {}, {}
    held = None
    for step in range(1, far + 2):
        at = step - 1
        p_got, q_got = p_in, q_in
        if step <= far:
            last = step == far
            p_in = move(p_got[:half] if last else p_got, out_ring)
            q_in = move(q_got[half:] if last else q_got, back_ring)
        if at == 0:
            (own, other), held = load_and_mlp(
                [p_got, move(p_got, pair)], sel, w_gate, w_up, w_down
            )
            own_sib = move(other, pair)
            done = (own, other)
        else:
            p_sib, q_sib = move(p_got, pair), move(q_got, pair)
            blocks = [p_got, q_sib, p_sib, q_got]
            n = p_got.shape[0]
            if at == far:
                out_rows = (2 * n, 2 * n)
                segments = ((0, 0, 0, 2 * n), (1, 0, 2 * n, 2 * n))
            else:
                out_rows = (n, n, 2 * n)
                segments = (
                    (0, 0, 0, half), (0, half, n + half, half),
                    (1, 0, half, half), (1, half, n, half),
                    (2, 0, 2 * n, half), (2, half, 3 * n + half, half),
                    (2, n, 2 * n + half, half), (2, n + half, 3 * n, half),
                )
            done = mlp(blocks, sel, *held, out_rows, segments)
            mine_a[at], other = done[0], done[-1]
            if at < far:
                mine_b[at] = done[1]
            sib[at] = move(other, pair)
        if step <= far:
            p_in, q_in, *rest = lax.optimization_barrier((p_in, q_in) + tuple(done))

    first, second = (), ()
    attention_out = None
    for d in range(far - 1, -1, -1):
        if d > 0:
            total = total_of(*second, mine_b[d], sib[d][count:])
            total, sib[d] = lax.optimization_barrier((total, sib[d]))
            if d == 5:
                total, queries = lax.optimization_barrier((total, queries))
                attention_out = decode_attention(queries, key_cache, cached_value_rows, lengths)
            second = (move(total, back_ring),)
        e = d + 1
        total = total_of(*first, mine_a[e], sib[e][:count])
        if d == 2:
            total, attention_out = lax.optimization_barrier((total, attention_out))
        first = (move(total, back_ring),)
    top = move(second[0][half:], pair)
    bottom = move(first[0][half:], pair)
    moe_out = jnp.concatenate([
        total_of(own[:half], own_sib[:half], first[0][:half], top),
        total_of(own[half:], own_sib[half:], second[0][:half], bottom),
    ], axis=0)
    return (moe_out, attention_out)


def solution(mesh):
    in_specs = (
        P(("group", "ep"), None),
        P(("group", "ep"), None),
        P(),
        P(None, "ep"),
        P(None, "ep"),
        P("ep", None),
        P(("group", "ep"), None, None),
        P(("group", "ep"), None, None, None),
        P(("group", "ep"), None, None, None),
        P(("group", "ep")),
    )
    out_specs = (P(("group", "ep"), None), P(("group", "ep"), None, None))

    return jax.shard_map(
        on_device, mesh=mesh, in_specs=in_specs, out_specs=out_specs, check_vma=False
    )
```

time: 344 us -> 230 us (0.67)
  waiting for transfers between devices: 233 us -> 42.5 us
  starting transfers between devices: 0.13 us -> 91.8 us
  matrix products: 77.3 us -> 4.79 us
  Pallas kernels: 0 us -> 66.9 us
  between operations: 14.2 us -> 1.04 us
  other arithmetic: 10.1 us -> 15.6 us
    reduce_scatter x1 -> x0, waiting for transfers between devices: 142 us -> none  [on_device(): lax.psum_scatter(terms.reshape(token_count * lax.axis_size('ep'), feature...]
    ppermute x0 -> x59, starting transfers between devices: none -> 91.8 us  [move(): return lax.ppermute(v, 'ep', pairs)]
    all_gather x1 -> x0, waiting for transfers between devices: 91 us -> none  [sent_together(): lax.all_gather(both, axis, axis=dim, tiled=True)]
    dot_general x5 -> x1, matrix products: 74.5 us -> 1.35 us  [gate_table(): logits = jnp.dot(tokens, w_router, preferred_element_type=jnp.float32)]
    pallas_call x0 -> x9, Pallas kernels: none -> 66.9 us  [the longest x8 56.9 us: mlp(): pl.pallas_call(functools.partial(mlp_body, n, len(out_rows), segments, up...]
    ppermute x0 -> x59, waiting for transfers between devices: none -> 42.5 us  [move(): return lax.ppermute(v, 'ep', pairs)]
    convert_element_type x3 -> x17, other arithmetic: 3.88 us -> 13.1 us  [the longest x16 13.1 us: total_of(): return acc.astype(jnp.bfloat16)]
    split x1 -> x0, local copies, waits for them, and re-layouts: 6.24 us -> none  [sent_together(): jnp.split(lax.all_gather(both, axis, axis=dim, tiled=True), ends, axis=al...]
  transfers between devices with their start and end apart: 2 -> 59, of which waited for: 2 -> 22; matrix products, arithmetic and copies ran while one was open for 1% -> 8% of each run, Pallas kernels for 0% -> 27%
where the time goes in v1:
time: 230 us; the launch traced here: 229 us
  starting transfers between devices  91.8 us (40%)
  Pallas kernels  66.9 us (29%)
  waiting for transfers between devices  42.5 us (18%)
  other arithmetic  15.6 us (7%)
  local copies, waits for them, and re-layouts  6.14 us (3%)
  matrix products  4.79 us (2%)
    ppermute x59, starting transfers between devices, move(): return lax.ppermute(v, 'ep', pairs)  91.8 us
    pallas_call x8, Pallas kernels, mlp(): pl.pallas_call(functools.partial(mlp_body, n, len(out_rows), segments, up...  56.9 us
    ppermute x59, waiting for transfers between devices, move(): return lax.ppermute(v, 'ep', pairs)  42.5 us
    convert_element_type x16, other arithmetic, total_of(): return acc.astype(jnp.bfloat16)  13.1 us
    pallas_call x1, Pallas kernels, load_and_mlp(): pl.pallas_call(functools.partial(load_body, n, rows, parts), in_specs=[vm...  9.98 us
  transfers between devices with their start and end apart: 59, of which 22 were waited for; matrix products, arithmetic and copies ran while one was open for 8% of the time, Pallas kernels for 27%

profile of v1, /device:TPU:70, one launch (start us, length us, event | category | flops | bytes accessed | tf_op | source)
XLA Modules:
  0.0 228.7 jit_solution(3384485493127177151)
XLA Ops:
  5.0 12.6 %collective-permute-start.3 = (bf16[64,3200]{1,0:T(8,128)(2,1)S(1)}, bf16[64,3200]{1,0:T(8,128)(2,1)S(1)}, u32[]{:S(2)}, u32[]{:S(2)}) collective-permute-start(bf16[64,3200]{1,0:T(8,128)(2,1)S(1)} %concatenate.9.refs_0_), channel_id=1, source_target_pairs={{0,30},{1,3},{2,0},{3,5},{4,2},{5,7},{6,4},{7,9},{8,6},{9,11},{10,... | collective-permute-start | bytes 1228808 | tf_op jit(solution)/shard_map/ppermute | solution.py:217
  17.7 10.0 %load_and_mlp.1 = (bf16[64,3072]{1,0:T(8,128)(2,1)S(1)}, bf16[64,3072]{1,0:T(8,128)(2,1)S(1)}, bf16[3072,1024]{1,0:T(8,128)(2,1)S(1)}, bf16[3072,1024]{1,0:T(8,128)(2,1)S(1)}, bf16[1024,3072]{1,0:T(8,128)(2,1)S(1)}) custom-call(bf16[64,3200]{1,0:T(8,128)(2,1)S(1)} %concatenate.9.refs_0_, bf16[64,3200]{1,0:T(8,128)(2,1)} %collective-permute-done.refs_1_, ...), custom_call_target="tpu_custom_call" | custom-call | flops 2415919104 | bytes 18874368 | tf_op jit(solution)/shard_map/load_and_mlp/pallas_call | solution.py:136
  28.3 3.2 %collective-permute-start.5 = (bf16[64,3200]{1,0:T(8,128)(2,1)S(1)}, bf16[64,3200]{1,0:T(8,128)(2,1)S(1)}, u32[]{:S(2)}, u32[]{:S(2)}) collective-permute-start(bf16[64,3200]{1,0:T(8,128)(2,1)S(1)} %collective-permute-done.3.refs_3_), channel_id=1, source_target_pairs={{0,30},{1,3},{2,0},{3,5},{4,2},{5,7},{6,4},{7,9},{8,6},{9,11},{10,... | collective-permute-start | bytes 1228808 | tf_op jit(solution)/shard_map/ppermute | solution.py:217
  31.6 7.9 %mlp.8 = (bf16[64,3072]{1,0:T(8,128)(2,1)S(1)}, bf16[64,3072]{1,0:T(8,128)(2,1)S(1)}, bf16[128,3072]{1,0:T(8,128)(2,1)}) custom-call(bf16[64,3200]{1,0:T(8,128)(2,1)S(1)} %collective-permute-done.2.refs_0_, bf16[64,3200]{1,0:T(8,128)(2,1)S(1)} %collective-permute-done.6.refs_1_, bf16[64,3200]{1,0:T(8,128)(2,1)S(1)} %collective-permute-done.7.refs_2_, ...), custom_call_target="tpu_custom_call" | custom-call | flops 4831838208 | bytes 18874368 | tf_op jit(solution)/shard_map/mlp/pallas_call | solution.py:62
  41.7 3.2 %collective-permute-start.9 = (bf16[64,3200]{1,0:T(8,128)(2,1)S(1)}, bf16[64,3200]{1,0:T(8,128)(2,1)S(1)}, u32[]{:S(2)}, u32[]{:S(2)}) collective-permute-start(bf16[64,3200]{1,0:T(8,128)(2,1)S(1)} %collective-permute-done.5.refs_3_), channel_id=1, source_target_pairs={{0,30},{1,3},{2,0},{3,5},{4,2},{5,7},{6,4},{7,9},{8,6},{9,11},{10,... | collective-permute-start | bytes 1228808 | tf_op jit(solution)/shard_map/ppermute | solution.py:217
  45.0 7.8 %mlp.9 = (bf16[64,3072]{1,0:T(8,128)(2,1)S(1)}, bf16[64,3072]{1,0:T(8,128)(2,1)S(1)}, bf16[128,3072]{1,0:T(8,128)(2,1)}) custom-call(bf16[64,3200]{1,0:T(8,128)(2,1)S(1)} %collective-permute-done.4.refs_0_, bf16[64,3200]{1,0:T(8,128)(2,1)S(1)} %collective-permute-done.10.refs_1_, bf16[64,3200]{1,0:T(8,128)(2,1)S(1)} %collective-permute-done.11.refs_2_, ...), custom_call_target="tpu_custom_call" | custom-call | flops 4831838208 | bytes 18874368 | tf_op jit(solution)/shard_map/mlp/pallas_call | solution.py:62
  55.1 3.2 %collective-permute-start.13 = (bf16[64,3200]{1,0:T(8,128)(2,1)S(1)}, bf16[64,3200]{1,0:T(8,128)(2,1)S(1)}, u32[]{:S(2)}, u32[]{:S(2)}) collective-permute-start(bf16[64,3200]{1,0:T(8,128)(2,1)S(1)} %collective-permute-done.9.refs_3_), channel_id=1, source_target_pairs={{0,30},{1,3},{2,0},{3,5},{4,2},{5,7},{6,4},{7,9},{8,6},{9,11},{10,... | collective-permute-start | bytes 1228808 | tf_op jit(solution)/shard_map/ppermute | solution.py:217
  58.3 7.8 %mlp.10 = (bf16[64,3072]{1,0:T(8,128)(2,1)S(1)}, bf16[64,3072]{1,0:T(8,128)(2,1)S(1)}, bf16[128,3072]{1,0:T(8,128)(2,1)}) custom-call(bf16[64,3200]{1,0:T(8,128)(2,1)S(1)} %collective-permute-done.8.refs_0_, bf16[64,3200]{1,0:T(8,128)(2,1)S(1)} %collective-permute-done.14.refs_1_, bf16[64,3200]{1,0:T(8,128)(2,1)S(1)} %collective-permute-done.15.refs_2_, ...), custom_call_target="tpu_custom_call" | custom-call | flops 4831838208 | bytes 18874368 | tf_op jit(solution)/shard_map/mlp/pallas_call | solution.py:62
  68.5 3.2 %collective-permute-start.17 = (bf16[64,3200]{1,0:T(8,128)(2,1)S(1)}, bf16[64,3200]{1,0:T(8,128)(2,1)S(1)}, u32[]{:S(2)}, u32[]{:S(2)}) collective-permute-start(bf16[64,3200]{1,0:T(8,128)(2,1)S(1)} %collective-permute-done.13.refs_3_), channel_id=1, source_target_pairs={{0,30},{1,3},{2,0},{3,5},{4,2},{5,7},{6,4},{7,9},{8,6},{9,11},{10,... | collective-permute-start | bytes 1228808 | tf_op jit(solution)/shard_map/ppermute | solution.py:217
  71.7 7.8 %mlp.11 = (bf16[64,3072]{1,0:T(8,128)(2,1)S(1)}, bf16[64,3072]{1,0:T(8,128)(2,1)S(1)}, bf16[128,3072]{1,0:T(8,128)(2,1)}) custom-call(bf16[64,3200]{1,0:T(8,128)(2,1)S(1)} %collective-permute-done.12.refs_0_, bf16[64,3200]{1,0:T(8,128)(2,1)S(1)} %collective-permute-done.18.refs_1_, bf16[64,3200]{1,0:T(8,128)(2,1)S(1)} %collective-permute-done.19.refs_2_, ...), custom_call_target="tpu_custom_call" | custom-call | flops 4831838208 | bytes 18874368 | tf_op jit(solution)/shard_map/mlp/pallas_call | solution.py:62
  81.8 3.2 %collective-permute-start.21 = (bf16[64,3200]{1,0:T(8,128)(2,1)S(1)}, bf16[64,3200]{1,0:T(8,128)(2,1)S(1)}, u32[]{:S(2)}, u32[]{:S(2)}) collective-permute-start(bf16[64,3200]{1,0:T(8,128)(2,1)S(1)} %collective-permute-done.17.refs_3_), channel_id=1, source_target_pairs={{0,30},{1,3},{2,0},{3,5},{4,2},{5,7},{6,4},{7,9},{8,6},{9,11},{10,... | collective-permute-start | bytes 1228808 | tf_op jit(solution)/shard_map/ppermute | solution.py:217
  85.1 6.9 %mlp.12 = (bf16[64,3072]{1,0:T(8,128)(2,1)S(1)}, bf16[64,3072]{1,0:T(8,128)(2,1)S(1)}, bf16[128,3072]{1,0:T(8,128)(2,1)S(1)}) custom-call(bf16[64,3200]{1,0:T(8,128)(2,1)S(1)} %collective-permute-done.16.refs_0_, bf16[64,3200]{1,0:T(8,128)(2,1)S(1)} %collective-permute-done.22.refs_1_, bf16[64,3200]{1,0:T(8,128)(2,1)S(1)} %collective-permute-done.23.refs_2_, ...), custom_call_target="tpu_custom_call" | custom-call | flops 4831838208 | bytes 18874368 | tf_op jit(solution)/shard_map/mlp/pallas_call | solution.py:62
  95.2 3.2 %collective-permute-start.25 = (bf16[64,3200]{1,0:T(8,128)(2,1)S(1)}, bf16[64,3200]{1,0:T(8,128)(2,1)S(1)}, u32[]{:S(2)}, u32[]{:S(2)}) collective-permute-start(bf16[64,3200]{1,0:T(8,128)(2,1)S(1)} %collective-permute-done.21.refs_3_), channel_id=1, source_target_pairs={{0,30},{1,3},{2,0},{3,5},{4,2},{5,7},{6,4},{7,9},{8,6},{9,11},{10,... | collective-permute-start | bytes 1228808 | tf_op jit(solution)/shard_map/ppermute | solution.py:217
  98.5 6.9 %mlp.13 = (bf16[64,3072]{1,0:T(8,128)(2,1)S(1)}, bf16[64,3072]{1,0:T(8,128)(2,1)S(1)}, bf16[128,3072]{1,0:T(8,128)(2,1)S(1)}) custom-call(bf16[64,3200]{1,0:T(8,128)(2,1)S(1)} %collective-permute-done.20.refs_0_, bf16[64,3200]{1,0:T(8,128)(2,1)S(1)} %collective-permute-done.26.refs_1_, bf16[64,3200]{1,0:T(8,128)(2,1)S(1)} %collective-permute-done.27.refs_2_, ...), custom_call_target="tpu_custom_call" | custom-call | flops 4831838208 | bytes 18874368 | tf_op jit(solution)/shard_map/mlp/pallas_call | solution.py:62
  110.8 6.9 %mlp.14 = (bf16[64,3072]{1,0:T(8,128)(2,1)S(1)}, bf16[64,3072]{1,0:T(8,128)(2,1)S(1)}, bf16[128,3072]{1,0:T(8,128)(2,1)S(1)}) custom-call(bf16[64,3200]{1,0:T(8,128)(2,1)S(1)} %collective-permute-done.24.refs_0_, bf16[64,3200]{1,0:T(8,128)(2,1)S(1)} %collective-permute-done.30.refs_1_, bf16[64,3200]{1,0:T(8,128)(2,1)S(1)} %collective-permute-done.31.refs_2_, ...), custom_call_target="tpu_custom_call" | custom-call | flops 4831838208 | bytes 18874368 | tf_op jit(solution)/shard_map/mlp/pallas_call | solution.py:62
  120.5 4.6 %mlp.15 = (bf16[64,3072]{1,0:T(8,128)(2,1)S(1)}, bf16[64,3072]{1,0:T(8,128)(2,1)S(1)}) custom-call(bf16[32,3200]{1,0:T(8,128)(2,1)S(1)} %collective-permute-done.28.refs_0_, bf16[32,3200]{1,0:T(8,128)(2,1)S(1)} %collective-permute-done.32.refs_1_, bf16[32,3200]{1,0:T(8,128)(2,1)S(1)} %collective-permute-done.33.refs_2_, ...), custom_call_target="tpu_custom_call" | custom-call | flops 2415919104 | bytes 18874368 | tf_op jit(solution)/shard_map/mlp/pallas_call | solution.py:62
  130.2 5.7 %collective-permute-done.35 = bf16[64,3072]{1,0:T(8,128)(2,1)S(1)} collective-permute-done((bf16[64,3072]{1,0:T(8,128)(2,1)S(1)}, bf16[64,3072]{1,0:T(8,128)(2,1)S(1)}, u32[]{:S(2)}, u32[]{:S(2)}) %collective-permute-start.35) | collective-permute-done | bytes 393248 | tf_op jit(solution)/shard_map/ppermute | solution.py:217
  135.9 3.2 %collective-permute-start.38 = (bf16[64,3072]{1,0:T(8,128)(2,1)S(1)}, bf16[64,3072]{1,0:T(8,128)(2,1)S(1)}, u32[]{:S(2)}, u32[]{:S(2)}) collective-permute-start(bf16[64,3072]{1,0:T(8,128)(2,1)S(1)} %add_convert_fusion.13), channel_id=1, source_target_pairs={{0,30},{1,3},{2,0},{3,5},{4,2},{5,7},{6,4},{7,9},{8,6},{9,11},{10,... | collective-permute-start | bytes 1179656 | tf_op jit(solution)/shard_map/ppermute | solution.py:217
  139.4 5.0 %collective-permute-done.38 = bf16[64,3072]{1,0:T(8,128)(2,1)S(1)} collective-permute-done((bf16[64,3072]{1,0:T(8,128)(2,1)S(1)}, bf16[64,3072]{1,0:T(8,128)(2,1)S(1)}, u32[]{:S(2)}, u32[]{:S(2)}) %collective-permute-start.38) | collective-permute-done | bytes 393248 | tf_op jit(solution)/shard_map/ppermute | solution.py:217
  144.4 3.7 %collective-permute-start.37 = (bf16[64,3072]{1,0:T(8,128)(2,1)S(1)}, bf16[64,3072]{1,0:T(8,128)(2,1)S(1)}, u32[]{:S(2)}, u32[]{:S(2)}) collective-permute-start(bf16[64,3072]{1,0:T(8,128)(2,1)S(1)} %add_convert_fusion.12), channel_id=1, source_target_pairs={{0,30},{1,3},{2,0},{3,5},{4,2},{5,7},{6,4},{7,9},{8,6},{9,11},{10,... | collective-permute-start | bytes 1179656 | tf_op jit(solution)/shard_map/ppermute | solution.py:217
  148.3 5.1 %collective-permute-done.37 = bf16[64,3072]{1,0:T(8,128)(2,1)S(1)} collective-permute-done((bf16[64,3072]{1,0:T(8,128)(2,1)S(1)}, bf16[64,3072]{1,0:T(8,128)(2,1)S(1)}, u32[]{:S(2)}, u32[]{:S(2)}) %collective-permute-start.37) | collective-permute-done | bytes 393248 | tf_op jit(solution)/shard_map/ppermute | solution.py:217
  153.4 3.7 %collective-permute-start.41 = (bf16[64,3072]{1,0:T(8,128)(2,1)S(1)}, bf16[64,3072]{1,0:T(8,128)(2,1)S(1)}, u32[]{:S(2)}, u32[]{:S(2)}) collective-permute-start(bf16[64,3072]{1,0:T(8,128)(2,1)S(1)} %add_convert_fusion.11), channel_id=1, source_target_pairs={{0,30},{1,3},{2,0},{3,5},{4,2},{5,7},{6,4},{7,9},{8,6},{9,11},{10,... | collective-permute-start | bytes 1179656 | tf_op jit(solution)/shard_map/ppermute | solution.py:217
  158.0 4.4 %collective-permute-done.41 = bf16[64,3072]{1,0:T(8,128)(2,1)S(1)} collective-permute-done((bf16[64,3072]{1,0:T(8,128)(2,1)S(1)}, bf16[64,3072]{1,0:T(8,128)(2,1)S(1)}, u32[]{:S(2)}, u32[]{:S(2)}) %collective-permute-start.41) | collective-permute-done | bytes 393248 | tf_op jit(solution)/shard_map/ppermute | solution.py:217
  162.4 3.7 %collective-permute-start.40 = (bf16[64,3072]{1,0:T(8,128)(2,1)}, bf16[64,3072]{1,0:T(8,128)(2,1)}, u32[]{:S(2)}, u32[]{:S(2)}) collective-permute-start(bf16[64,3072]{1,0:T(8,128)(2,1)} %add_convert_fusion.10), channel_id=1, source_target_pairs={{0,30},{1,3},{2,0},{3,5},{4,2},{5,7},{6,4},{7,9},{8,6},{9,11},{10,... | collective-permute-start | bytes 1179656 | tf_op jit(solution)/shard_map/ppermute | solution.py:217
  171.7 3.7 %collective-permute-start.44 = (bf16[64,3072]{1,0:T(8,128)(2,1)}, bf16[64,3072]{1,0:T(8,128)(2,1)S(1)}, u32[]{:S(2)}, u32[]{:S(2)}) collective-permute-start(bf16[64,3072]{1,0:T(8,128)(2,1)} %add_convert_fusion.9), channel_id=1, source_target_pairs={{0,30},{1,3},{2,0},{3,5},{4,2},{5,7},{6,4},{7,9},{8,6},{9,11},{10,... | collective-permute-start | bytes 1179656 | tf_op jit(solution)/shard_map/ppermute | solution.py:217
  176.9 4.1 %collective-permute-done.44 = bf16[64,3072]{1,0:T(8,128)(2,1)S(1)} collective-permute-done((bf16[64,3072]{1,0:T(8,128)(2,1)}, bf16[64,3072]{1,0:T(8,128)(2,1)S(1)}, u32[]{:S(2)}, u32[]{:S(2)}) %collective-permute-start.44) | collective-permute-done | bytes 393248 | tf_op jit(solution)/shard_map/ppermute | solution.py:217
  182.3 3.7 %collective-permute-start.47 = (bf16[64,3072]{1,0:T(8,128)(2,1)S(1)}, bf16[64,3072]{1,0:T(8,128)(2,1)S(1)}, u32[]{:S(2)}, u32[]{:S(2)}) collective-permute-start(bf16[64,3072]{1,0:T(8,128)(2,1)S(1)} %add_convert_fusion.7), channel_id=1, source_target_pairs={{0,30},{1,3},{2,0},{3,5},{4,2},{5,7},{6,4},{7,9},{8,6},{9,11},{10,... | collective-permute-start | bytes 1179656 | tf_op jit(solution)/shard_map/ppermute | solution.py:217
  192.4 3.8 %collective-permute-start.50 = (bf16[64,3072]{1,0:T(8,128)(2,1)S(1)}, bf16[64,3072]{1,0:T(8,128)(2,1)S(1)}, u32[]{:S(2)}, u32[]{:S(2)}) collective-permute-start(bf16[64,3072]{1,0:T(8,128)(2,1)S(1)} %add_convert_fusion.5), channel_id=1, source_target_pairs={{0,30},{1,3},{2,0},{3,5},{4,2},{5,7},{6,4},{7,9},{8,6},{9,11},{10,... | collective-permute-start | bytes 1179656 | tf_op jit(solution)/shard_map/ppermute | solution.py:217
  202.6 3.8 %collective-permute-start.53 = (bf16[64,3072]{1,0:T(8,128)(2,1)S(1)}, bf16[64,3072]{1,0:T(8,128)(2,1)S(1)}, u32[]{:S(2)}, u32[]{:S(2)}) collective-permute-start(bf16[64,3072]{1,0:T(8,128)(2,1)S(1)} %add_convert_fusion.3), channel_id=1, source_target_pairs={{0,30},{1,3},{2,0},{3,5},{4,2},{5,7},{6,4},{7,9},{8,6},{9,11},{10,... | collective-permute-start | bytes 1179656 | tf_op jit(solution)/shard_map/ppermute | solution.py:217
  212.9 3.8 %collective-permute-start.56 = (bf16[64,3072]{1,0:T(8,128)(2,1)S(1)}, bf16[64,3072]{1,0:T(8,128)(2,1)S(1)}, u32[]{:S(2)}, u32[]{:S(2)}) collective-permute-start(bf16[64,3072]{1,0:T(8,128)(2,1)S(1)} %add_convert_fusion.1), channel_id=1, source_target_pairs={{0,30},{1,3},{2,0},{3,5},{4,2},{5,7},{6,4},{7,9},{8,6},{9,11},{10,... | collective-permute-start | bytes 1179656 | tf_op jit(solution)/shard_map/ppermute | solution.py:217
  217.8 3.1 %collective-permute-start.55 = (bf16[64,3072]{1,0:T(8,128)(2,1)S(1)}, bf16[64,3072]{1,0:T(8,128)(2,1)S(1)}, u32[]{:S(2)}, u32[]{:S(2)}) collective-permute-start(bf16[64,3072]{1,0:T(8,128)(2,1)S(1)} %add_convert_fusion), channel_id=1, source_target_pairs={{0,30},{1,3},{2,0},{3,5},{4,2},{5,7},{6,4},{7,9},{8,6},{9,11},{10,... | collective-permute-start | bytes 1179656 | tf_op jit(solution)/shard_map/ppermute | solution.py:217
  222.1 4.1 %collective-permute-done.55 = bf16[64,3072]{1,0:T(8,128)(2,1)S(1)} collective-permute-done((bf16[64,3072]{1,0:T(8,128)(2,1)S(1)}, bf16[64,3072]{1,0:T(8,128)(2,1)S(1)}, u32[]{:S(2)}, u32[]{:S(2)}) %collective-permute-start.55) | collective-permute-done | bytes 393248 | tf_op jit(solution)/shard_map/ppermute | solution.py:217
  (173 shorter events, 64.3 us)
Async XLA Ops:
  4.9 12.8 %collective-permute-start = (bf16[64,3200]{1,0:T(8,128)(2,1)S(1)}, bf16[64,3200]{1,0:T(8,128)(2,1)}, u32[]{:S(2)}, u32[]{:S(2)}) collective-permute-start(bf16[64,3200]{1,0:T(8,128)(2,1)S(1)} %concatenate.9.refs_0_), channel_id=1, source_target_pairs={{0,1},{1,0},{2,3},{3,2},{4,5},{5,4},{6,7},{7,6},{8,9},{9,8},{10,11... | collective-permute-start | bytes 1228808 | tf_op jit(solution)/shard_map/ppermute | solution.py:217
  5.0 22.7 %collective-permute-start.3 = (bf16[64,3200]{1,0:T(8,128)(2,1)S(1)}, bf16[64,3200]{1,0:T(8,128)(2,1)S(1)}, u32[]{:S(2)}, u32[]{:S(2)}) collective-permute-start(bf16[64,3200]{1,0:T(8,128)(2,1)S(1)} %concatenate.9.refs_0_), channel_id=1, source_target_pairs={{0,30},{1,3},{2,0},{3,5},{4,2},{5,7},{6,4},{7,9},{8,6},{9,11},{10,... | collective-permute-start | bytes 1228808 | tf_op jit(solution)/shard_map/ppermute | solution.py:217
  17.7 10.0 %collective-permute-start.2 = (bf16[64,3200]{1,0:T(8,128)(2,1)S(1)}, bf16[64,3200]{1,0:T(8,128)(2,1)S(1)}, u32[]{:S(2)}, u32[]{:S(2)}) collective-permute-start(bf16[64,3200]{1,0:T(8,128)(2,1)S(1)} %concatenate.9.refs_0_), channel_id=1, source_target_pairs={{0,2},{1,31},{2,4},{3,1},{4,6},{5,3},{6,8},{7,5},{8,10},{9,7},{10,... | collective-permute-start | bytes 1228808 | tf_op jit(solution)/shard_map/ppermute | solution.py:217
  28.3 12.7 %collective-permute-start.4 = (bf16[64,3200]{1,0:T(8,128)(2,1)S(1)}, bf16[64,3200]{1,0:T(8,128)(2,1)S(1)}, u32[]{:S(2)}, u32[]{:S(2)}) collective-permute-start(bf16[64,3200]{1,0:T(8,128)(2,1)S(1)} %collective-permute-done.2.refs_0_), channel_id=1, source_target_pairs={{0,2},{1,31},{2,4},{3,1},{4,6},{5,3},{6,8},{7,5},{8,10},{9,7},{10,... | collective-permute-start | bytes 1228808 | tf_op jit(solution)/shard_map/ppermute | solution.py:217
  28.3 12.7 %collective-permute-start.5 = (bf16[64,3200]{1,0:T(8,128)(2,1)S(1)}, bf16[64,3200]{1,0:T(8,128)(2,1)S(1)}, u32[]{:S(2)}, u32[]{:S(2)}) collective-permute-start(bf16[64,3200]{1,0:T(8,128)(2,1)S(1)} %collective-permute-done.3.refs_3_), channel_id=1, source_target_pairs={{0,30},{1,3},{2,0},{3,5},{4,2},{5,7},{6,4},{7,9},{8,6},{9,11},{10,... | collective-permute-start | bytes 1228808 | tf_op jit(solution)/shard_map/ppermute | solution.py:217
  41.7 11.7 %collective-permute-start.8 = (bf16[64,3200]{1,0:T(8,128)(2,1)S(1)}, bf16[64,3200]{1,0:T(8,128)(2,1)S(1)}, u32[]{:S(2)}, u32[]{:S(2)}) collective-permute-start(bf16[64,3200]{1,0:T(8,128)(2,1)S(1)} %collective-permute-done.4.refs_0_), channel_id=1, source_target_pairs={{0,2},{1,31},{2,4},{3,1},{4,6},{5,3},{6,8},{7,5},{8,10},{9,7},{10,... | collective-permute-start | bytes 1228808 | tf_op jit(solution)/shard_map/ppermute | solution.py:217
  41.7 12.0 %collective-permute-start.9 = (bf16[64,3200]{1,0:T(8,128)(2,1)S(1)}, bf16[64,3200]{1,0:T(8,128)(2,1)S(1)}, u32[]{:S(2)}, u32[]{:S(2)}) collective-permute-start(bf16[64,3200]{1,0:T(8,128)(2,1)S(1)} %collective-permute-done.5.refs_3_), channel_id=1, source_target_pairs={{0,30},{1,3},{2,0},{3,5},{4,2},{5,7},{6,4},{7,9},{8,6},{9,11},{10,... | collective-permute-start | bytes 1228808 | tf_op jit(solution)/shard_map/ppermute | solution.py:217
  55.1 12.0 %collective-permute-start.12 = (bf16[64,3200]{1,0:T(8,128)(2,1)S(1)}, bf16[64,3200]{1,0:T(8,128)(2,1)S(1)}, u32[]{:S(2)}, u32[]{:S(2)}) collective-permute-start(bf16[64,3200]{1,0:T(8,128)(2,1)S(1)} %collective-permute-done.8.refs_0_), channel_id=1, source_target_pairs={{0,2},{1,31},{2,4},{3,1},{4,6},{5,3},{6,8},{7,5},{8,10},{9,7},{10,... | collective-permute-start | bytes 1228808 | tf_op jit(solution)/shard_map/ppermute | solution.py:217
  55.1 12.0 %collective-permute-start.13 = (bf16[64,3200]{1,0:T(8,128)(2,1)S(1)}, bf16[64,3200]{1,0:T(8,128)(2,1)S(1)}, u32[]{:S(2)}, u32[]{:S(2)}) collective-permute-start(bf16[64,3200]{1,0:T(8,128)(2,1)S(1)} %collective-permute-done.9.refs_3_), channel_id=1, source_target_pairs={{0,30},{1,3},{2,0},{3,5},{4,2},{5,7},{6,4},{7,9},{8,6},{9,11},{10,... | collective-permute-start | bytes 1228808 | tf_op jit(solution)/shard_map/ppermute | solution.py:217
  68.5 12.3 %collective-permute-start.16 = (bf16[64,3200]{1,0:T(8,128)(2,1)S(1)}, bf16[64,3200]{1,0:T(8,128)(2,1)S(1)}, u32[]{:S(2)}, u32[]{:S(2)}) collective-permute-start(bf16[64,3200]{1,0:T(8,128)(2,1)S(1)} %collective-permute-done.12.refs_0_), channel_id=1, source_target_pairs={{0,2},{1,31},{2,4},{3,1},{4,6},{5,3},{6,8},{7,5},{8,10},{9,7},{10,... | collective-permute-start | bytes 1228808 | tf_op jit(solution)/shard_map/ppermute | solution.py:217
  68.5 12.3 %collective-permute-start.17 = (bf16[64,3200]{1,0:T(8,128)(2,1)S(1)}, bf16[64,3200]{1,0:T(8,128)(2,1)S(1)}, u32[]{:S(2)}, u32[]{:S(2)}) collective-permute-start(bf16[64,3200]{1,0:T(8,128)(2,1)S(1)} %collective-permute-done.13.refs_3_), channel_id=1, source_target_pairs={{0,30},{1,3},{2,0},{3,5},{4,2},{5,7},{6,4},{7,9},{8,6},{9,11},{10,... | collective-permute-start | bytes 1228808 | tf_op jit(solution)/shard_map/ppermute | solution.py:217
  81.8 12.6 %collective-permute-start.20 = (bf16[64,3200]{1,0:T(8,128)(2,1)S(1)}, bf16[64,3200]{1,0:T(8,128)(2,1)S(1)}, u32[]{:S(2)}, u32[]{:S(2)}) collective-permute-start(bf16[64,3200]{1,0:T(8,128)(2,1)S(1)} %collective-permute-done.16.refs_0_), channel_id=1, source_target_pairs={{0,2},{1,31},{2,4},{3,1},{4,6},{5,3},{6,8},{7,5},{8,10},{9,7},{10,... | collective-permute-start | bytes 1228808 | tf_op jit(solution)/shard_map/ppermute | solution.py:217
  81.8 12.6 %collective-permute-start.21 = (bf16[64,3200]{1,0:T(8,128)(2,1)S(1)}, bf16[64,3200]{1,0:T(8,128)(2,1)S(1)}, u32[]{:S(2)}, u32[]{:S(2)}) collective-permute-start(bf16[64,3200]{1,0:T(8,128)(2,1)S(1)} %collective-permute-done.17.refs_3_), channel_id=1, source_target_pairs={{0,30},{1,3},{2,0},{3,5},{4,2},{5,7},{6,4},{7,9},{8,6},{9,11},{10,... | collective-permute-start | bytes 1228808 | tf_op jit(solution)/shard_map/ppermute | solution.py:217
  95.2 12.8 %collective-permute-start.24 = (bf16[64,3200]{1,0:T(8,128)(2,1)S(1)}, bf16[64,3200]{1,0:T(8,128)(2,1)S(1)}, u32[]{:S(2)}, u32[]{:S(2)}) collective-permute-start(bf16[64,3200]{1,0:T(8,128)(2,1)S(1)} %collective-permute-done.20.refs_0_), channel_id=1, source_target_pairs={{0,2},{1,31},{2,4},{3,1},{4,6},{5,3},{6,8},{7,5},{8,10},{9,7},{10,... | collective-permute-start | bytes 1228808 | tf_op jit(solution)/shard_map/ppermute | solution.py:217
  95.2 12.8 %collective-permute-start.25 = (bf16[64,3200]{1,0:T(8,128)(2,1)S(1)}, bf16[64,3200]{1,0:T(8,128)(2,1)S(1)}, u32[]{:S(2)}, u32[]{:S(2)}) collective-permute-start(bf16[64,3200]{1,0:T(8,128)(2,1)S(1)} %collective-permute-done.21.refs_3_), channel_id=1, source_target_pairs={{0,30},{1,3},{2,0},{3,5},{4,2},{5,7},{6,4},{7,9},{8,6},{9,11},{10,... | collective-permute-start | bytes 1228808 | tf_op jit(solution)/shard_map/ppermute | solution.py:217
  108.6 9.1 %collective-permute-start.29 = (bf16[32,3200]{1,0:T(8,128)(2,1)S(1)}, bf16[32,3200]{1,0:T(8,128)(2,1)S(1)}, u32[]{:S(2)}, u32[]{:S(2)}) collective-permute-start(bf16[32,3200]{1,0:T(8,128)(2,1)S(1)} %slice.75), channel_id=1, source_target_pairs={{0,30},{1,3},{2,0},{3,5},{4,2},{5,7},{6,4},{7,9},{8,6},{9,11},{10,... | collective-permute-start | bytes 614408 | tf_op jit(solution)/shard_map/ppermute | solution.py:217
  125.8 84.8 %collective-permute-start.54 = (bf16[128,3072]{1,0:T(8,128)(2,1)}, bf16[128,3072]{1,0:T(8,128)(2,1)}, u32[]{:S(2)}, u32[]{:S(2)}) collective-permute-start(bf16[128,3072]{1,0:T(8,128)(2,1)} %get-tuple-element.73), channel_id=1, source_target_pairs={{0,1},{1,0},{2,3},{3,2},{4,5},{5,4},{6,7},{7,6},{8,9},{9,8},{10,11... | collective-permute-start | bytes 2359304 | tf_op jit(solution)/shard_map/ppermute | solution.py:217
  126.2 74.2 %collective-permute-start.51 = (bf16[128,3072]{1,0:T(8,128)(2,1)}, bf16[128,3072]{1,0:T(8,128)(2,1)}, u32[]{:S(2)}, u32[]{:S(2)}) collective-permute-start(bf16[128,3072]{1,0:T(8,128)(2,1)} %get-tuple-element.78), channel_id=1, source_target_pairs={{0,1},{1,0},{2,3},{3,2},{4,5},{5,4},{6,7},{7,6},{8,9},{9,8},{10,11... | collective-permute-start | bytes 2359304 | tf_op jit(solution)/shard_map/ppermute | solution.py:217
  126.4 63.6 %collective-permute-start.48 = (bf16[128,3072]{1,0:T(8,128)(2,1)}, bf16[128,3072]{1,0:T(8,128)(2,1)}, u32[]{:S(2)}, u32[]{:S(2)}) collective-permute-start(bf16[128,3072]{1,0:T(8,128)(2,1)} %get-tuple-element.83), channel_id=1, source_target_pairs={{0,1},{1,0},{2,3},{3,2},{4,5},{5,4},{6,7},{7,6},{8,9},{9,8},{10,11... | collective-permute-start | bytes 2359304 | tf_op jit(solution)/shard_map/ppermute | solution.py:217
  127.0 12.3 %collective-permute-start.39 = (bf16[128,3072]{1,0:T(8,128)(2,1)S(1)}, bf16[128,3072]{1,0:T(8,128)(2,1)S(1)}, u32[]{:S(2)}, u32[]{:S(2)}) collective-permute-start(bf16[128,3072]{1,0:T(8,128)(2,1)S(1)} %get-tuple-element.98), channel_id=1, source_target_pairs={{0,1},{1,0},{2,3},{3,2},{4,5},{5,4},{6,7},{7,6},{8,9},{9,8},{10,11... | collective-permute-start | bytes 2359304 | tf_op jit(solution)/shard_map/ppermute | solution.py:217
  139.3 18.7 %collective-permute-start.42 = (bf16[128,3072]{1,0:T(8,128)(2,1)S(1)}, bf16[128,3072]{1,0:T(8,128)(2,1)S(1)}, u32[]{:S(2)}, u32[]{:S(2)}) collective-permute-start(bf16[128,3072]{1,0:T(8,128)(2,1)S(1)} %get-tuple-element.93), channel_id=1, source_target_pairs={{0,1},{1,0},{2,3},{3,2},{4,5},{5,4},{6,7},{7,6},{8,9},{9,8},{10,11... | collective-permute-start | bytes 2359304 | tf_op jit(solution)/shard_map/ppermute | solution.py:217
  144.4 9.0 %collective-permute-start.37 = (bf16[64,3072]{1,0:T(8,128)(2,1)S(1)}, bf16[64,3072]{1,0:T(8,128)(2,1)S(1)}, u32[]{:S(2)}, u32[]{:S(2)}) collective-permute-start(bf16[64,3072]{1,0:T(8,128)(2,1)S(1)} %add_convert_fusion.12), channel_id=1, source_target_pairs={{0,30},{1,3},{2,0},{3,5},{4,2},{5,7},{6,4},{7,9},{8,6},{9,11},{10,... | collective-permute-start | bytes 1179656 | tf_op jit(solution)/shard_map/ppermute | solution.py:217
  158.0 18.8 %collective-permute-start.45 = (bf16[128,3072]{1,0:T(8,128)(2,1)}, bf16[128,3072]{1,0:T(8,128)(2,1)}, u32[]{:S(2)}, u32[]{:S(2)}) collective-permute-start(bf16[128,3072]{1,0:T(8,128)(2,1)} %get-tuple-element.88), channel_id=1, source_target_pairs={{0,1},{1,0},{2,3},{3,2},{4,5},{5,4},{6,7},{7,6},{8,9},{9,8},{10,11... | collective-permute-start | bytes 2359304 | tf_op jit(solution)/shard_map/ppermute | solution.py:217
  162.4 9.3 %collective-permute-start.40 = (bf16[64,3072]{1,0:T(8,128)(2,1)}, bf16[64,3072]{1,0:T(8,128)(2,1)}, u32[]{:S(2)}, u32[]{:S(2)}) collective-permute-start(bf16[64,3072]{1,0:T(8,128)(2,1)} %add_convert_fusion.10), channel_id=1, source_target_pairs={{0,30},{1,3},{2,0},{3,5},{4,2},{5,7},{6,4},{7,9},{8,6},{9,11},{10,... | collective-permute-start | bytes 1179656 | tf_op jit(solution)/shard_map/ppermute | solution.py:217
  171.7 9.3 %collective-permute-start.44 = (bf16[64,3072]{1,0:T(8,128)(2,1)}, bf16[64,3072]{1,0:T(8,128)(2,1)S(1)}, u32[]{:S(2)}, u32[]{:S(2)}) collective-permute-start(bf16[64,3072]{1,0:T(8,128)(2,1)} %add_convert_fusion.9), channel_id=1, source_target_pairs={{0,30},{1,3},{2,0},{3,5},{4,2},{5,7},{6,4},{7,9},{8,6},{9,11},{10,... | collective-permute-start | bytes 1179656 | tf_op jit(solution)/shard_map/ppermute | solution.py:217
  176.8 9.2 %collective-permute-start.43 = (bf16[64,3072]{1,0:T(8,128)(2,1)S(1)}, bf16[64,3072]{1,0:T(8,128)(2,1)S(1)}, u32[]{:S(2)}, u32[]{:S(2)}) collective-permute-start(bf16[64,3072]{1,0:T(8,128)(2,1)S(1)} %add_convert_fusion.8), channel_id=1, source_target_pairs={{0,30},{1,3},{2,0},{3,5},{4,2},{5,7},{6,4},{7,9},{8,6},{9,11},{10,... | collective-permute-start | bytes 1179656 | tf_op jit(solution)/shard_map/ppermute | solution.py:217
  187.1 9.1 %collective-permute-start.46 = (bf16[64,3072]{1,0:T(8,128)(2,1)S(1)}, bf16[64,3072]{1,0:T(8,128)(2,1)S(1)}, u32[]{:S(2)}, u32[]{:S(2)}) collective-permute-start(bf16[64,3072]{1,0:T(8,128)(2,1)S(1)} %add_convert_fusion.6), channel_id=1, source_target_pairs={{0,30},{1,3},{2,0},{3,5},{4,2},{5,7},{6,4},{7,9},{8,6},{9,11},{10,... | collective-permute-start | bytes 1179656 | tf_op jit(solution)/shard_map/ppermute | solution.py:217
  192.4 9.1 %collective-permute-start.50 = (bf16[64,3072]{1,0:T(8,128)(2,1)S(1)}, bf16[64,3072]{1,0:T(8,128)(2,1)S(1)}, u32[]{:S(2)}, u32[]{:S(2)}) collective-permute-start(bf16[64,3072]{1,0:T(8,128)(2,1)S(1)} %add_convert_fusion.5), channel_id=1, source_target_pairs={{0,30},{1,3},{2,0},{3,5},{4,2},{5,7},{6,4},{7,9},{8,6},{9,11},{10,... | collective-permute-start | bytes 1179656 | tf_op jit(solution)/shard_map/ppermute | solution.py:217
  197.3 9.1 %collective-permute-start.49 = (bf16[64,3072]{1,0:T(8,128)(2,1)S(1)}, bf16[64,3072]{1,0:T(8,128)(2,1)S(1)}, u32[]{:S(2)}, u32[]{:S(2)}) collective-permute-start(bf16[64,3072]{1,0:T(8,128)(2,1)S(1)} %add_convert_fusion.4), channel_id=1, source_target_pairs={{0,30},{1,3},{2,0},{3,5},{4,2},{5,7},{6,4},{7,9},{8,6},{9,11},{10,... | collective-permute-start | bytes 1179656 | tf_op jit(solution)/shard_map/ppermute | solution.py:217
  202.6 9.1 %collective-permute-start.53 = (bf16[64,3072]{1,0:T(8,128)(2,1)S(1)}, bf16[64,3072]{1,0:T(8,128)(2,1)S(1)}, u32[]{:S(2)}, u32[]{:S(2)}) collective-permute-start(bf16[64,3072]{1,0:T(8,128)(2,1)S(1)} %add_convert_fusion.3), channel_id=1, source_target_pairs={{0,30},{1,3},{2,0},{3,5},{4,2},{5,7},{6,4},{7,9},{8,6},{9,11},{10,... | collective-permute-start | bytes 1179656 | tf_op jit(solution)/shard_map/ppermute | solution.py:217
  207.6 9.1 %collective-permute-start.52 = (bf16[64,3072]{1,0:T(8,128)(2,1)S(1)}, bf16[64,3072]{1,0:T(8,128)(2,1)S(1)}, u32[]{:S(2)}, u32[]{:S(2)}) collective-permute-start(bf16[64,3072]{1,0:T(8,128)(2,1)S(1)} %add_convert_fusion.2), channel_id=1, source_target_pairs={{0,30},{1,3},{2,0},{3,5},{4,2},{5,7},{6,4},{7,9},{8,6},{9,11},{10,... | collective-permute-start | bytes 1179656 | tf_op jit(solution)/shard_map/ppermute | solution.py:217
  212.9 9.1 %collective-permute-start.56 = (bf16[64,3072]{1,0:T(8,128)(2,1)S(1)}, bf16[64,3072]{1,0:T(8,128)(2,1)S(1)}, u32[]{:S(2)}, u32[]{:S(2)}) collective-permute-start(bf16[64,3072]{1,0:T(8,128)(2,1)S(1)} %add_convert_fusion.1), channel_id=1, source_target_pairs={{0,30},{1,3},{2,0},{3,5},{4,2},{5,7},{6,4},{7,9},{8,6},{9,11},{10,... | collective-permute-start | bytes 1179656 | tf_op jit(solution)/shard_map/ppermute | solution.py:217
  (45 other events, 482.1 us)

commit v2 on v1

--- a/solution.py
+++ b/solution.py
@@ -11,7 +11,7 @@
 PAD = 128
 VMEM_LIMIT = 8 * 2**20
 LOAD_LIMIT = 30 * 2**20
-AHEAD = 2
+AHEAD = 3
 
 
 def store_rows(outs, y, gate, cols, segments):
@@ -164,7 +164,7 @@
     return jnp.sum(jnp.where(onehot, gate_values[:, :, None], jnp.float32(0.0)), axis=1)
 
 
-def decode_attention(queries, key_cache, cached_value_rows, lengths):
+def attention_weights(queries, key_cache, lengths):
     request_count, head_count, head_dim = queries.shape
     cache_len = key_cache.shape[1]
     kv_heads = key_cache.shape[2]
@@ -176,11 +176,15 @@
     scores = jnp.where(visible[:, None, None, :], scores, -jnp.inf)
     row_max = jnp.max(scores, axis=3, keepdims=True)
     exponent = jnp.exp(scores - row_max)
-    weights = (exponent / jnp.sum(exponent, axis=3, keepdims=True)).astype(jnp.bfloat16)
+    return (exponent / jnp.sum(exponent, axis=3, keepdims=True)).astype(jnp.bfloat16)
+
+
+def attention_mix(weights, cached_value_rows):
     mixed = jnp.einsum(
         "bkgl,blkd->bkgd", weights, cached_value_rows, preferred_element_type=jnp.float32
     )
-    return mixed.reshape(request_count, head_count, head_dim).astype(jnp.bfloat16)
+    request_count, kv_heads, group, head_dim = mixed.shape
+    return mixed.reshape(request_count, kv_heads * group, head_dim).astype(jnp.bfloat16)
 
 
 def total_of(*parts):
@@ -265,27 +269,33 @@
         if step <= far:
             p_in, q_in, *rest = lax.optimization_barrier((p_in, q_in) + tuple(done))
 
+    own_total = own.astype(jnp.float32) + own_sib.astype(jnp.float32)
     first, second = (), ()
-    attention_out = None
+    weights = None
     for d in range(far - 1, -1, -1):
         if d > 0:
             total = total_of(*second, mine_b[d], sib[d][count:])
             total, sib[d] = lax.optimization_barrier((total, sib[d]))
-            if d == 5:
+            if d == 2:
+                total, own_total = lax.optimization_barrier((total, own_total))
+            if d == 1:
                 total, queries = lax.optimization_barrier((total, queries))
-                attention_out = decode_attention(queries, key_cache, cached_value_rows, lengths)
+                weights = attention_weights(queries, key_cache, lengths)
             second = (move(total, back_ring),)
         e = d + 1
+        if d == 0:
+            *first, weights = lax.optimization_barrier((*first, weights))
         total = total_of(*first, mine_a[e], sib[e][:count])
-        if d == 2:
-            total, attention_out = lax.optimization_barrier((total, attention_out))
         first = (move(total, back_ring),)
+    attention_out = attention_mix(weights, cached_value_rows)
+    *first, attention_out = lax.optimization_barrier((*first, attention_out))
     top = move(second[0][half:], pair)
     bottom = move(first[0][half:], pair)
-    moe_out = jnp.concatenate([
-        total_of(own[:half], own_sib[:half], first[0][:half], top),
-        total_of(own[half:], own_sib[half:], second[0][:half], bottom),
-    ], axis=0)
+    moe_out = total_of(
+        own_total,
+        jnp.concatenate([first[0][:half], second[0][:half]], axis=0),
+        jnp.concatenate([top, bottom], axis=0),
+    )
     return (moe_out, attention_out)
 
 

time: 230 us -> 226 us (0.983)
  waiting for transfers between devices: 42.5 us -> 52.8 us
  other arithmetic: 15.6 us -> 7.18 us
  Pallas kernels: 66.9 us -> 62.3 us
    ppermute x59, waiting for transfers between devices: 42.5 us -> 52.8 us  [move(): return lax.ppermute(v, 'ep', pairs)]
    convert_element_type x16, other arithmetic: 13.1 us -> 5.58 us  [total_of(): return acc.astype(jnp.bfloat16)]
    pallas_call x8, Pallas kernels: 56.9 us -> 53.3 us  [mlp(): pl.pallas_call(functools.partial(mlp_body, n, len(out_rows), segments, up...]
    unnamed x37 -> x13, local copies, waits for them, and re-layouts: 3.73 us -> 1.4 us
  transfers between devices with their start and end apart: 59 -> 59, of which waited for: 22 -> 25; matrix products, arithmetic and copies ran while one was open for 8% -> 4% of each run, Pallas kernels for 27% -> 28%
where the time goes in v2:
time: 226 us; the launch traced here: 225 us
  starting transfers between devices  93.2 us (41%)
  Pallas kernels  62.3 us (28%)
  waiting for transfers between devices  52.8 us (23%)
  other arithmetic  7.18 us (3%)
  matrix products  4.13 us (2%)
  local copies, waits for them, and re-layouts  3.98 us (2%)
    ppermute x59, starting transfers between devices, move(): return lax.ppermute(v, 'ep', pairs)  93.2 us
    pallas_call x8, Pallas kernels, mlp(): pl.pallas_call(functools.partial(mlp_body, n, len(out_rows), segments, up...  53.3 us
    ppermute x59, waiting for transfers between devices, move(): return lax.ppermute(v, 'ep', pairs)  52.8 us
    pallas_call x1, Pallas kernels, load_and_mlp(): pl.pallas_call(functools.partial(load_body, n, rows, parts), in_specs=[vm...  8.92 us
    convert_element_type x16, other arithmetic, total_of(): return acc.astype(jnp.bfloat16)  5.58 us
  transfers between devices with their start and end apart: 59, of which 25 were waited for; matrix products, arithmetic and copies ran while one was open for 4% of the time, Pallas kernels for 28%

profile of v2, /device:TPU:70, one launch (start us, length us, event | category | flops | bytes accessed | tf_op | source)
XLA Modules:
  0.0 224.6 jit_solution(6425417405739153050)
XLA Ops:
  7.2 10.5 %collective-permute-start.1 = (bf16[64,3200]{1,0:T(8,128)(2,1)S(1)}, bf16[64,3200]{1,0:T(8,128)(2,1)S(1)}, u32[]{:S(2)}, u32[]{:S(2)}) collective-permute-start(bf16[64,3200]{1,0:T(8,128)(2,1)S(1)} %concatenate.12.refs_0_), channel_id=1, source_target_pairs={{0,30},{1,3},{2,0},{3,5},{4,2},{5,7},{6,4},{7,9},{8,6},{9,11},{10,... | collective-permute-start | bytes 1228808 | tf_op jit(solution)/shard_map/ppermute | solution.py:221
  17.8 8.9 %load_and_mlp.1 = (bf16[64,3072]{1,0:T(8,128)(2,1)S(1)}, bf16[64,3072]{1,0:T(8,128)(2,1)S(1)}, bf16[3072,1024]{1,0:T(8,128)(2,1)S(1)}, bf16[3072,1024]{1,0:T(8,128)(2,1)S(1)}, bf16[1024,3072]{1,0:T(8,128)(2,1)S(1)}) custom-call(bf16[64,3200]{1,0:T(8,128)(2,1)S(1)} %concatenate.12.refs_0_, bf16[64,3200]{1,0:T(8,128)(2,1)} %collective-permute-done.2.refs_1_, ...), custom_call_target="tpu_custom_call" | custom-call | flops 2415919104 | bytes 18874368 | tf_op jit(solution)/shard_map/load_and_mlp/pallas_call | solution.py:136
  27.8 3.3 %collective-permute-start.4 = (bf16[64,3200]{1,0:T(8,128)(2,1)S(1)}, bf16[64,3200]{1,0:T(8,128)(2,1)S(1)}, u32[]{:S(2)}, u32[]{:S(2)}) collective-permute-start(bf16[64,3200]{1,0:T(8,128)(2,1)S(1)} %collective-permute-done.1.refs_3_), channel_id=1, source_target_pairs={{0,30},{1,3},{2,0},{3,5},{4,2},{5,7},{6,4},{7,9},{8,6},{9,11},{10,... | collective-permute-start | bytes 1228808 | tf_op jit(solution)/shard_map/ppermute | solution.py:221
  31.1 7.0 %mlp.8 = (bf16[64,3072]{1,0:T(8,128)(2,1)S(1)}, bf16[64,3072]{1,0:T(8,128)(2,1)S(1)}, bf16[128,3072]{1,0:T(8,128)(2,1)S(1)}) custom-call(bf16[64,3200]{1,0:T(8,128)(2,1)S(1)} %collective-permute-done.refs_0_, bf16[64,3200]{1,0:T(8,128)(2,1)S(1)} %collective-permute-done.5.refs_1_, bf16[64,3200]{1,0:T(8,128)(2,1)S(1)} %collective-permute-done.6.refs_2_, ...), custom_call_target="tpu_custom_call" | custom-call | flops 4831838208 | bytes 18874368 | tf_op jit(solution)/shard_map/mlp/pallas_call | solution.py:62
  41.3 3.2 %collective-permute-start.8 = (bf16[64,3200]{1,0:T(8,128)(2,1)S(1)}, bf16[64,3200]{1,0:T(8,128)(2,1)S(1)}, u32[]{:S(2)}, u32[]{:S(2)}) collective-permute-start(bf16[64,3200]{1,0:T(8,128)(2,1)S(1)} %collective-permute-done.4.refs_3_), channel_id=1, source_target_pairs={{0,30},{1,3},{2,0},{3,5},{4,2},{5,7},{6,4},{7,9},{8,6},{9,11},{10,... | collective-permute-start | bytes 1228808 | tf_op jit(solution)/shard_map/ppermute | solution.py:221
  44.5 6.9 %mlp.9 = (bf16[64,3072]{1,0:T(8,128)(2,1)S(1)}, bf16[64,3072]{1,0:T(8,128)(2,1)S(1)}, bf16[128,3072]{1,0:T(8,128)(2,1)S(1)}) custom-call(bf16[64,3200]{1,0:T(8,128)(2,1)S(1)} %collective-permute-done.3.refs_0_, bf16[64,3200]{1,0:T(8,128)(2,1)S(1)} %collective-permute-done.9.refs_1_, bf16[64,3200]{1,0:T(8,128)(2,1)S(1)} %collective-permute-done.10.refs_2_, ...), custom_call_target="tpu_custom_call" | custom-call | flops 4831838208 | bytes 18874368 | tf_op jit(solution)/shard_map/mlp/pallas_call | solution.py:62
  54.6 3.2 %collective-permute-start.12 = (bf16[64,3200]{1,0:T(8,128)(2,1)S(1)}, bf16[64,3200]{1,0:T(8,128)(2,1)S(1)}, u32[]{:S(2)}, u32[]{:S(2)}) collective-permute-start(bf16[64,3200]{1,0:T(8,128)(2,1)S(1)} %collective-permute-done.8.refs_3_), channel_id=1, source_target_pairs={{0,30},{1,3},{2,0},{3,5},{4,2},{5,7},{6,4},{7,9},{8,6},{9,11},{10,... | collective-permute-start | bytes 1228808 | tf_op jit(solution)/shard_map/ppermute | solution.py:221
  57.9 6.9 %mlp.10 = (bf16[64,3072]{1,0:T(8,128)(2,1)S(1)}, bf16[64,3072]{1,0:T(8,128)(2,1)S(1)}, bf16[128,3072]{1,0:T(8,128)(2,1)S(1)}) custom-call(bf16[64,3200]{1,0:T(8,128)(2,1)S(1)} %collective-permute-done.7.refs_0_, bf16[64,3200]{1,0:T(8,128)(2,1)S(1)} %collective-permute-done.13.refs_1_, bf16[64,3200]{1,0:T(8,128)(2,1)S(1)} %collective-permute-done.14.refs_2_, ...), custom_call_target="tpu_custom_call" | custom-call | flops 4831838208 | bytes 18874368 | tf_op jit(solution)/shard_map/mlp/pallas_call | solution.py:62
  68.0 3.2 %collective-permute-start.16 = (bf16[64,3200]{1,0:T(8,128)(2,1)S(1)}, bf16[64,3200]{1,0:T(8,128)(2,1)S(1)}, u32[]{:S(2)}, u32[]{:S(2)}) collective-permute-start(bf16[64,3200]{1,0:T(8,128)(2,1)S(1)} %collective-permute-done.12.refs_3_), channel_id=1, source_target_pairs={{0,30},{1,3},{2,0},{3,5},{4,2},{5,7},{6,4},{7,9},{8,6},{9,11},{10,... | collective-permute-start | bytes 1228808 | tf_op jit(solution)/shard_map/ppermute | solution.py:221
  71.3 6.9 %mlp.11 = (bf16[64,3072]{1,0:T(8,128)(2,1)S(1)}, bf16[64,3072]{1,0:T(8,128)(2,1)S(1)}, bf16[128,3072]{1,0:T(8,128)(2,1)S(1)}) custom-call(bf16[64,3200]{1,0:T(8,128)(2,1)S(1)} %collective-permute-done.11.refs_0_, bf16[64,3200]{1,0:T(8,128)(2,1)S(1)} %collective-permute-done.17.refs_1_, bf16[64,3200]{1,0:T(8,128)(2,1)S(1)} %collective-permute-done.18.refs_2_, ...), custom_call_target="tpu_custom_call" | custom-call | flops 4831838208 | bytes 18874368 | tf_op jit(solution)/shard_map/mlp/pallas_call | solution.py:62
  81.4 3.2 %collective-permute-start.20 = (bf16[64,3200]{1,0:T(8,128)(2,1)S(1)}, bf16[64,3200]{1,0:T(8,128)(2,1)S(1)}, u32[]{:S(2)}, u32[]{:S(2)}) collective-permute-start(bf16[64,3200]{1,0:T(8,128)(2,1)S(1)} %collective-permute-done.16.refs_3_), channel_id=1, source_target_pairs={{0,30},{1,3},{2,0},{3,5},{4,2},{5,7},{6,4},{7,9},{8,6},{9,11},{10,... | collective-permute-start | bytes 1228808 | tf_op jit(solution)/shard_map/ppermute | solution.py:221
  84.6 6.9 %mlp.12 = (bf16[64,3072]{1,0:T(8,128)(2,1)S(1)}, bf16[64,3072]{1,0:T(8,128)(2,1)S(1)}, bf16[128,3072]{1,0:T(8,128)(2,1)S(1)}) custom-call(bf16[64,3200]{1,0:T(8,128)(2,1)S(1)} %collective-permute-done.15.refs_0_, bf16[64,3200]{1,0:T(8,128)(2,1)S(1)} %collective-permute-done.21.refs_1_, bf16[64,3200]{1,0:T(8,128)(2,1)S(1)} %collective-permute-done.22.refs_2_, ...), custom_call_target="tpu_custom_call" | custom-call | flops 4831838208 | bytes 18874368 | tf_op jit(solution)/shard_map/mlp/pallas_call | solution.py:62
  98.0 7.0 %mlp.13 = (bf16[64,3072]{1,0:T(8,128)(2,1)S(1)}, bf16[64,3072]{1,0:T(8,128)(2,1)S(1)}, bf16[128,3072]{1,0:T(8,128)(2,1)S(1)}) custom-call(bf16[64,3200]{1,0:T(8,128)(2,1)S(1)} %collective-permute-done.19.refs_0_, bf16[64,3200]{1,0:T(8,128)(2,1)S(1)} %collective-permute-done.25.refs_1_, bf16[64,3200]{1,0:T(8,128)(2,1)S(1)} %collective-permute-done.26.refs_2_, ...), custom_call_target="tpu_custom_call" | custom-call | flops 4831838208 | bytes 18874368 | tf_op jit(solution)/shard_map/mlp/pallas_call | solution.py:62
  112.1 6.9 %mlp.14 = (bf16[64,3072]{1,0:T(8,128)(2,1)S(1)}, bf16[64,3072]{1,0:T(8,128)(2,1)S(1)}, bf16[128,3072]{1,0:T(8,128)(2,1)S(1)}) custom-call(bf16[64,3200]{1,0:T(8,128)(2,1)S(1)} %collective-permute-done.23.refs_0_, bf16[64,3200]{1,0:T(8,128)(2,1)S(1)} %collective-permute-done.27.refs_1_, bf16[64,3200]{1,0:T(8,128)(2,1)S(1)} %collective-permute-done.28.refs_2_, ...), custom_call_target="tpu_custom_call" | custom-call | flops 4831838208 | bytes 18874368 | tf_op jit(solution)/shard_map/mlp/pallas_call | solution.py:62
  120.9 4.6 %mlp.15 = (bf16[64,3072]{1,0:T(8,128)(2,1)S(1)}, bf16[64,3072]{1,0:T(8,128)(2,1)S(1)}) custom-call(bf16[32,3200]{1,0:T(8,128)(2,1)S(1)} %collective-permute-done.41.refs_0_, bf16[32,3200]{1,0:T(8,128)(2,1)S(1)} %collective-permute-done.43.refs_1_, bf16[32,3200]{1,0:T(8,128)(2,1)S(1)} %collective-permute-done.44.refs_2_, ...), custom_call_target="tpu_custom_call" | custom-call | flops 2415919104 | bytes 18874368 | tf_op jit(solution)/shard_map/mlp/pallas_call | solution.py:62
  128.7 6.9 %collective-permute-done.46 = bf16[64,3072]{1,0:T(8,128)(2,1)S(1)} collective-permute-done((bf16[64,3072]{1,0:T(8,128)(2,1)S(1)}, bf16[64,3072]{1,0:T(8,128)(2,1)S(1)}, u32[]{:S(2)}, u32[]{:S(2)}) %collective-permute-start.46) | collective-permute-done | bytes 393248 | tf_op jit(solution)/shard_map/ppermute | solution.py:221
  137.9 5.5 %collective-permute-done.30 = bf16[64,3072]{1,0:T(8,128)(2,1)S(1)} collective-permute-done((bf16[64,3072]{1,0:T(8,128)(2,1)S(1)}, bf16[64,3072]{1,0:T(8,128)(2,1)S(1)}, u32[]{:S(2)}, u32[]{:S(2)}) %collective-permute-start.30) | collective-permute-done | bytes 393248 | tf_op jit(solution)/shard_map/ppermute | solution.py:221
  146.7 5.1 %collective-permute-done.47 = bf16[64,3072]{1,0:T(8,128)(2,1)S(1)} collective-permute-done((bf16[64,3072]{1,0:T(8,128)(2,1)S(1)}, bf16[64,3072]{1,0:T(8,128)(2,1)S(1)}, u32[]{:S(2)}, u32[]{:S(2)}) %collective-permute-start.47) | collective-permute-done | bytes 393248 | tf_op jit(solution)/shard_map/ppermute | solution.py:221
  151.9 3.7 %collective-permute-start.32 = (bf16[64,3072]{1,0:T(8,128)(2,1)S(1)}, bf16[64,3072]{1,0:T(8,128)(2,1)S(1)}, u32[]{:S(2)}, u32[]{:S(2)}) collective-permute-start(bf16[64,3072]{1,0:T(8,128)(2,1)S(1)} %add_convert_fusion.14), channel_id=1, source_target_pairs={{0,30},{1,3},{2,0},{3,5},{4,2},{5,7},{6,4},{7,9},{8,6},{9,11},{10,... | collective-permute-start | bytes 1179656 | tf_op jit(solution)/shard_map/ppermute | solution.py:221
  155.9 5.0 %collective-permute-done.32 = bf16[64,3072]{1,0:T(8,128)(2,1)S(1)} collective-permute-done((bf16[64,3072]{1,0:T(8,128)(2,1)S(1)}, bf16[64,3072]{1,0:T(8,128)(2,1)S(1)}, u32[]{:S(2)}, u32[]{:S(2)}) %collective-permute-start.32) | collective-permute-done | bytes 393248 | tf_op jit(solution)/shard_map/ppermute | solution.py:221
  160.9 3.7 %collective-permute-start.48 = (bf16[64,3072]{1,0:T(8,128)(2,1)S(1)}, bf16[64,3072]{1,0:T(8,128)(2,1)S(1)}, u32[]{:S(2)}, u32[]{:S(2)}) collective-permute-start(bf16[64,3072]{1,0:T(8,128)(2,1)S(1)} %add_convert_fusion.7), channel_id=1, source_target_pairs={{0,30},{1,3},{2,0},{3,5},{4,2},{5,7},{6,4},{7,9},{8,6},{9,11},{10,... | collective-permute-start | bytes 1179656 | tf_op jit(solution)/shard_map/ppermute | solution.py:221
  164.7 5.1 %collective-permute-done.48 = bf16[64,3072]{1,0:T(8,128)(2,1)S(1)} collective-permute-done((bf16[64,3072]{1,0:T(8,128)(2,1)S(1)}, bf16[64,3072]{1,0:T(8,128)(2,1)S(1)}, u32[]{:S(2)}, u32[]{:S(2)}) %collective-permute-start.48) | collective-permute-done | bytes 393248 | tf_op jit(solution)/shard_map/ppermute | solution.py:221
  169.9 3.7 %collective-permute-start.34 = (bf16[64,3072]{1,0:T(8,128)(2,1)S(1)}, bf16[64,3072]{1,0:T(8,128)(2,1)S(1)}, u32[]{:S(2)}, u32[]{:S(2)}) collective-permute-start(bf16[64,3072]{1,0:T(8,128)(2,1)S(1)} %add_convert_fusion.13), channel_id=1, source_target_pairs={{0,30},{1,3},{2,0},{3,5},{4,2},{5,7},{6,4},{7,9},{8,6},{9,11},{10,... | collective-permute-start | bytes 1179656 | tf_op jit(solution)/shard_map/ppermute | solution.py:221
  173.8 5.0 %collective-permute-done.34 = bf16[64,3072]{1,0:T(8,128)(2,1)S(1)} collective-permute-done((bf16[64,3072]{1,0:T(8,128)(2,1)S(1)}, bf16[64,3072]{1,0:T(8,128)(2,1)S(1)}, u32[]{:S(2)}, u32[]{:S(2)}) %collective-permute-start.34) | collective-permute-done | bytes 393248 | tf_op jit(solution)/shard_map/ppermute | solution.py:221
  179.0 3.8 %collective-permute-start.36 = (bf16[64,3072]{1,0:T(8,128)(2,1)S(1)}, bf16[64,3072]{1,0:T(8,128)(2,1)S(1)}, u32[]{:S(2)}, u32[]{:S(2)}) collective-permute-start(bf16[64,3072]{1,0:T(8,128)(2,1)S(1)} %add_convert_fusion.12), channel_id=1, source_target_pairs={{0,30},{1,3},{2,0},{3,5},{4,2},{5,7},{6,4},{7,9},{8,6},{9,11},{10,... | collective-permute-start | bytes 1179656 | tf_op jit(solution)/shard_map/ppermute | solution.py:221
  183.2 3.8 %collective-permute-start.50 = (bf16[64,3072]{1,0:T(8,128)(2,1)S(1)}, bf16[64,3072]{1,0:T(8,128)(2,1)S(1)}, u32[]{:S(2)}, u32[]{:S(2)}) collective-permute-start(bf16[64,3072]{1,0:T(8,128)(2,1)S(1)} %add_convert_fusion.5), channel_id=1, source_target_pairs={{0,30},{1,3},{2,0},{3,5},{4,2},{5,7},{6,4},{7,9},{8,6},{9,11},{10,... | collective-permute-start | bytes 1179656 | tf_op jit(solution)/shard_map/ppermute | solution.py:221
  188.2 3.8 %collective-permute-start.38 = (bf16[64,3072]{1,0:T(8,128)(2,1)S(1)}, bf16[64,3072]{1,0:T(8,128)(2,1)S(1)}, u32[]{:S(2)}, u32[]{:S(2)}) collective-permute-start(bf16[64,3072]{1,0:T(8,128)(2,1)S(1)} %add_convert_fusion.11), channel_id=1, source_target_pairs={{0,30},{1,3},{2,0},{3,5},{4,2},{5,7},{6,4},{7,9},{8,6},{9,11},{10,... | collective-permute-start | bytes 1179656 | tf_op jit(solution)/shard_map/ppermute | solution.py:221
  192.5 3.8 %collective-permute-start.51 = (bf16[64,3072]{1,0:T(8,128)(2,1)S(1)}, bf16[64,3072]{1,0:T(8,128)(2,1)S(1)}, u32[]{:S(2)}, u32[]{:S(2)}) collective-permute-start(bf16[64,3072]{1,0:T(8,128)(2,1)S(1)} %add_convert_fusion.4), channel_id=1, source_target_pairs={{0,30},{1,3},{2,0},{3,5},{4,2},{5,7},{6,4},{7,9},{8,6},{9,11},{10,... | collective-permute-start | bytes 1179656 | tf_op jit(solution)/shard_map/ppermute | solution.py:221
  197.5 3.8 %collective-permute-start.53 = (bf16[64,3072]{1,0:T(8,128)(2,1)S(1)}, bf16[64,3072]{1,0:T(8,128)(2,1)S(1)}, u32[]{:S(2)}, u32[]{:S(2)}) collective-permute-start(bf16[64,3072]{1,0:T(8,128)(2,1)S(1)} %add_convert_fusion.10), channel_id=1, source_target_pairs={{0,30},{1,3},{2,0},{3,5},{4,2},{5,7},{6,4},{7,9},{8,6},{9,11},{10,... | collective-permute-start | bytes 1179656 | tf_op jit(solution)/shard_map/ppermute | solution.py:221
  202.5 3.7 %collective-permute-start.52 = (bf16[64,3072]{1,0:T(8,128)(2,1)}, bf16[64,3072]{1,0:T(8,128)(2,1)}, u32[]{:S(2)}, u32[]{:S(2)}) collective-permute-start(bf16[64,3072]{1,0:T(8,128)(2,1)} %add_convert_fusion.3), channel_id=1, source_target_pairs={{0,30},{1,3},{2,0},{3,5},{4,2},{5,7},{6,4},{7,9},{8,6},{9,11},{10,... | collective-permute-start | bytes 1179656 | tf_op jit(solution)/shard_map/ppermute | solution.py:221
  207.5 3.8 %collective-permute-start.56 = (bf16[64,3072]{1,0:T(8,128)(2,1)}, bf16[64,3072]{1,0:T(8,128)(2,1)}, u32[]{:S(2)}, u32[]{:S(2)}) collective-permute-start(bf16[64,3072]{1,0:T(8,128)(2,1)} %add_convert_fusion.2), channel_id=1, source_target_pairs={{0,30},{1,3},{2,0},{3,5},{4,2},{5,7},{6,4},{7,9},{8,6},{9,11},{10,... | collective-permute-start | bytes 1179656 | tf_op jit(solution)/shard_map/ppermute | solution.py:221
  213.4 3.4 %collective-permute-start.55 = (bf16[64,3072]{1,0:T(8,128)(2,1)S(1)}, bf16[64,3072]{1,0:T(8,128)(2,1)S(1)}, u32[]{:S(2)}, u32[]{:S(2)}) collective-permute-start(bf16[64,3072]{1,0:T(8,128)(2,1)S(1)} %add_convert_fusion.1), channel_id=1, source_target_pairs={{0,30},{1,3},{2,0},{3,5},{4,2},{5,7},{6,4},{7,9},{8,6},{9,11},{10,... | collective-permute-start | bytes 1179656 | tf_op jit(solution)/shard_map/ppermute | solution.py:221
  (148 shorter events, 60.9 us)
Async XLA Ops:
  4.9 12.9 %collective-permute-start.2 = (bf16[64,3200]{1,0:T(8,128)(2,1)S(1)}, bf16[64,3200]{1,0:T(8,128)(2,1)}, u32[]{:S(2)}, u32[]{:S(2)}) collective-permute-start(bf16[64,3200]{1,0:T(8,128)(2,1)S(1)} %concatenate.12.refs_0_), channel_id=1, source_target_pairs={{0,1},{1,0},{2,3},{3,2},{4,5},{5,4},{6,7},{7,6},{8,9},{9,8},{10,11... | collective-permute-start | bytes 1228808 | tf_op jit(solution)/shard_map/ppermute | solution.py:221
  5.0 21.7 %collective-permute-start = (bf16[64,3200]{1,0:T(8,128)(2,1)S(1)}, bf16[64,3200]{1,0:T(8,128)(2,1)S(1)}, u32[]{:S(2)}, u32[]{:S(2)}) collective-permute-start(bf16[64,3200]{1,0:T(8,128)(2,1)S(1)} %concatenate.12.refs_0_), channel_id=1, source_target_pairs={{0,2},{1,31},{2,4},{3,1},{4,6},{5,3},{6,8},{7,5},{8,10},{9,7},{10,... | collective-permute-start | bytes 1228808 | tf_op jit(solution)/shard_map/ppermute | solution.py:221
  7.2 19.7 %collective-permute-start.1 = (bf16[64,3200]{1,0:T(8,128)(2,1)S(1)}, bf16[64,3200]{1,0:T(8,128)(2,1)S(1)}, u32[]{:S(2)}, u32[]{:S(2)}) collective-permute-start(bf16[64,3200]{1,0:T(8,128)(2,1)S(1)} %concatenate.12.refs_0_), channel_id=1, source_target_pairs={{0,30},{1,3},{2,0},{3,5},{4,2},{5,7},{6,4},{7,9},{8,6},{9,11},{10,... | collective-permute-start | bytes 1228808 | tf_op jit(solution)/shard_map/ppermute | solution.py:221
  27.8 11.6 %collective-permute-start.3 = (bf16[64,3200]{1,0:T(8,128)(2,1)S(1)}, bf16[64,3200]{1,0:T(8,128)(2,1)S(1)}, u32[]{:S(2)}, u32[]{:S(2)}) collective-permute-start(bf16[64,3200]{1,0:T(8,128)(2,1)S(1)} %collective-permute-done.refs_0_), channel_id=1, source_target_pairs={{0,2},{1,31},{2,4},{3,1},{4,6},{5,3},{6,8},{7,5},{8,10},{9,7},{10,... | collective-permute-start | bytes 1228808 | tf_op jit(solution)/shard_map/ppermute | solution.py:221
  27.8 12.2 %collective-permute-start.4 = (bf16[64,3200]{1,0:T(8,128)(2,1)S(1)}, bf16[64,3200]{1,0:T(8,128)(2,1)S(1)}, u32[]{:S(2)}, u32[]{:S(2)}) collective-permute-start(bf16[64,3200]{1,0:T(8,128)(2,1)S(1)} %collective-permute-done.1.refs_3_), channel_id=1, source_target_pairs={{0,30},{1,3},{2,0},{3,5},{4,2},{5,7},{6,4},{7,9},{8,6},{9,11},{10,... | collective-permute-start | bytes 1228808 | tf_op jit(solution)/shard_map/ppermute | solution.py:221
  41.3 11.8 %collective-permute-start.7 = (bf16[64,3200]{1,0:T(8,128)(2,1)S(1)}, bf16[64,3200]{1,0:T(8,128)(2,1)S(1)}, u32[]{:S(2)}, u32[]{:S(2)}) collective-permute-start(bf16[64,3200]{1,0:T(8,128)(2,1)S(1)} %collective-permute-done.3.refs_0_), channel_id=1, source_target_pairs={{0,2},{1,31},{2,4},{3,1},{4,6},{5,3},{6,8},{7,5},{8,10},{9,7},{10,... | collective-permute-start | bytes 1228808 | tf_op jit(solution)/shard_map/ppermute | solution.py:221
  41.3 11.9 %collective-permute-start.8 = (bf16[64,3200]{1,0:T(8,128)(2,1)S(1)}, bf16[64,3200]{1,0:T(8,128)(2,1)S(1)}, u32[]{:S(2)}, u32[]{:S(2)}) collective-permute-start(bf16[64,3200]{1,0:T(8,128)(2,1)S(1)} %collective-permute-done.4.refs_3_), channel_id=1, source_target_pairs={{0,30},{1,3},{2,0},{3,5},{4,2},{5,7},{6,4},{7,9},{8,6},{9,11},{10,... | collective-permute-start | bytes 1228808 | tf_op jit(solution)/shard_map/ppermute | solution.py:221
  54.6 12.1 %collective-permute-start.11 = (bf16[64,3200]{1,0:T(8,128)(2,1)S(1)}, bf16[64,3200]{1,0:T(8,128)(2,1)S(1)}, u32[]{:S(2)}, u32[]{:S(2)}) collective-permute-start(bf16[64,3200]{1,0:T(8,128)(2,1)S(1)} %collective-permute-done.7.refs_0_), channel_id=1, source_target_pairs={{0,2},{1,31},{2,4},{3,1},{4,6},{5,3},{6,8},{7,5},{8,10},{9,7},{10,... | collective-permute-start | bytes 1228808 | tf_op jit(solution)/shard_map/ppermute | solution.py:221
  54.6 12.1 %collective-permute-start.12 = (bf16[64,3200]{1,0:T(8,128)(2,1)S(1)}, bf16[64,3200]{1,0:T(8,128)(2,1)S(1)}, u32[]{:S(2)}, u32[]{:S(2)}) collective-permute-start(bf16[64,3200]{1,0:T(8,128)(2,1)S(1)} %collective-permute-done.8.refs_3_), channel_id=1, source_target_pairs={{0,30},{1,3},{2,0},{3,5},{4,2},{5,7},{6,4},{7,9},{8,6},{9,11},{10,... | collective-permute-start | bytes 1228808 | tf_op jit(solution)/shard_map/ppermute | solution.py:221
  68.0 12.4 %collective-permute-start.15 = (bf16[64,3200]{1,0:T(8,128)(2,1)S(1)}, bf16[64,3200]{1,0:T(8,128)(2,1)S(1)}, u32[]{:S(2)}, u32[]{:S(2)}) collective-permute-start(bf16[64,3200]{1,0:T(8,128)(2,1)S(1)} %collective-permute-done.11.refs_0_), channel_id=1, source_target_pairs={{0,2},{1,31},{2,4},{3,1},{4,6},{5,3},{6,8},{7,5},{8,10},{9,7},{10,... | collective-permute-start | bytes 1228808 | tf_op jit(solution)/shard_map/ppermute | solution.py:221
  68.0 12.4 %collective-permute-start.16 = (bf16[64,3200]{1,0:T(8,128)(2,1)S(1)}, bf16[64,3200]{1,0:T(8,128)(2,1)S(1)}, u32[]{:S(2)}, u32[]{:S(2)}) collective-permute-start(bf16[64,3200]{1,0:T(8,128)(2,1)S(1)} %collective-permute-done.12.refs_3_), channel_id=1, source_target_pairs={{0,30},{1,3},{2,0},{3,5},{4,2},{5,7},{6,4},{7,9},{8,6},{9,11},{10,... | collective-permute-start | bytes 1228808 | tf_op jit(solution)/shard_map/ppermute | solution.py:221
  81.4 12.7 %collective-permute-start.19 = (bf16[64,3200]{1,0:T(8,128)(2,1)S(1)}, bf16[64,3200]{1,0:T(8,128)(2,1)S(1)}, u32[]{:S(2)}, u32[]{:S(2)}) collective-permute-start(bf16[64,3200]{1,0:T(8,128)(2,1)S(1)} %collective-permute-done.15.refs_0_), channel_id=1, source_target_pairs={{0,2},{1,31},{2,4},{3,1},{4,6},{5,3},{6,8},{7,5},{8,10},{9,7},{10,... | collective-permute-start | bytes 1228808 | tf_op jit(solution)/shard_map/ppermute | solution.py:221
  81.4 12.7 %collective-permute-start.20 = (bf16[64,3200]{1,0:T(8,128)(2,1)S(1)}, bf16[64,3200]{1,0:T(8,128)(2,1)S(1)}, u32[]{:S(2)}, u32[]{:S(2)}) collective-permute-start(bf16[64,3200]{1,0:T(8,128)(2,1)S(1)} %collective-permute-done.16.refs_3_), channel_id=1, source_target_pairs={{0,30},{1,3},{2,0},{3,5},{4,2},{5,7},{6,4},{7,9},{8,6},{9,11},{10,... | collective-permute-start | bytes 1228808 | tf_op jit(solution)/shard_map/ppermute | solution.py:221
  94.8 13.0 %collective-permute-start.23 = (bf16[64,3200]{1,0:T(8,128)(2,1)S(1)}, bf16[64,3200]{1,0:T(8,128)(2,1)S(1)}, u32[]{:S(2)}, u32[]{:S(2)}) collective-permute-start(bf16[64,3200]{1,0:T(8,128)(2,1)S(1)} %collective-permute-done.19.refs_0_), channel_id=1, source_target_pairs={{0,2},{1,31},{2,4},{3,1},{4,6},{5,3},{6,8},{7,5},{8,10},{9,7},{10,... | collective-permute-start | bytes 1228808 | tf_op jit(solution)/shard_map/ppermute | solution.py:221
  94.8 13.0 %collective-permute-start.24 = (bf16[64,3200]{1,0:T(8,128)(2,1)S(1)}, bf16[64,3200]{1,0:T(8,128)(2,1)S(1)}, u32[]{:S(2)}, u32[]{:S(2)}) collective-permute-start(bf16[64,3200]{1,0:T(8,128)(2,1)S(1)} %collective-permute-done.20.refs_3_), channel_id=1, source_target_pairs={{0,30},{1,3},{2,0},{3,5},{4,2},{5,7},{6,4},{7,9},{8,6},{9,11},{10,... | collective-permute-start | bytes 1228808 | tf_op jit(solution)/shard_map/ppermute | solution.py:221
  108.3 17.6 %collective-permute-start.40 = (bf16[64,3072]{1,0:T(8,128)(2,1)S(1)}, bf16[64,3072]{1,0:T(8,128)(2,1)S(1)}, u32[]{:S(2)}, u32[]{:S(2)}) collective-permute-start(bf16[64,3072]{1,0:T(8,128)(2,1)S(1)} %get-tuple-element.69), channel_id=1, source_target_pairs={{0,1},{1,0},{2,3},{3,2},{4,5},{5,4},{6,7},{7,6},{8,9},{9,8},{10,11... | collective-permute-start | bytes 1179656 | tf_op jit(solution)/shard_map/ppermute | solution.py:221
  108.7 10.3 %collective-permute-start.41 = (bf16[32,3200]{1,0:T(8,128)(2,1)S(1)}, bf16[32,3200]{1,0:T(8,128)(2,1)S(1)}, u32[]{:S(2)}, u32[]{:S(2)}) collective-permute-start(bf16[32,3200]{1,0:T(8,128)(2,1)S(1)} %slice.66), channel_id=1, source_target_pairs={{0,2},{1,31},{2,4},{3,1},{4,6},{5,3},{6,8},{7,5},{8,10},{9,7},{10,... | collective-permute-start | bytes 614408 | tf_op jit(solution)/shard_map/ppermute | solution.py:221
  108.8 10.2 %collective-permute-start.42 = (bf16[32,3200]{1,0:T(8,128)(2,1)S(1)}, bf16[32,3200]{1,0:T(8,128)(2,1)S(1)}, u32[]{:S(2)}, u32[]{:S(2)}) collective-permute-start(bf16[32,3200]{1,0:T(8,128)(2,1)S(1)} %slice.67), channel_id=1, source_target_pairs={{0,30},{1,3},{2,0},{3,5},{4,2},{5,7},{6,4},{7,9},{8,6},{9,11},{10,... | collective-permute-start | bytes 614408 | tf_op jit(solution)/shard_map/ppermute | solution.py:221
  126.0 80.2 %collective-permute-start.54 = (bf16[128,3072]{1,0:T(8,128)(2,1)S(1)}, bf16[128,3072]{1,0:T(8,128)(2,1)S(1)}, u32[]{:S(2)}, u32[]{:S(2)}) collective-permute-start(bf16[128,3072]{1,0:T(8,128)(2,1)S(1)} %get-tuple-element.77), channel_id=1, source_target_pairs={{0,1},{1,0},{2,3},{3,2},{4,5},{5,4},{6,7},{7,6},{8,9},{9,8},{10,11... | collective-permute-start | bytes 2359304 | tf_op jit(solution)/shard_map/ppermute | solution.py:221
  126.4 69.9 %collective-permute-start.39 = (bf16[128,3072]{1,0:T(8,128)(2,1)S(1)}, bf16[128,3072]{1,0:T(8,128)(2,1)S(1)}, u32[]{:S(2)}, u32[]{:S(2)}) collective-permute-start(bf16[128,3072]{1,0:T(8,128)(2,1)S(1)} %get-tuple-element.82), channel_id=1, source_target_pairs={{0,1},{1,0},{2,3},{3,2},{4,5},{5,4},{6,7},{7,6},{8,9},{9,8},{10,11... | collective-permute-start | bytes 2359304 | tf_op jit(solution)/shard_map/ppermute | solution.py:221
  126.6 60.4 %collective-permute-start.37 = (bf16[128,3072]{1,0:T(8,128)(2,1)S(1)}, bf16[128,3072]{1,0:T(8,128)(2,1)S(1)}, u32[]{:S(2)}, u32[]{:S(2)}) collective-permute-start(bf16[128,3072]{1,0:T(8,128)(2,1)S(1)} %get-tuple-element.87), channel_id=1, source_target_pairs={{0,1},{1,0},{2,3},{3,2},{4,5},{5,4},{6,7},{7,6},{8,9},{9,8},{10,11... | collective-permute-start | bytes 2359304 | tf_op jit(solution)/shard_map/ppermute | solution.py:221
  127.4 10.4 %collective-permute-start.31 = (bf16[128,3072]{1,0:T(8,128)(2,1)S(1)}, bf16[128,3072]{1,0:T(8,128)(2,1)S(1)}, u32[]{:S(2)}, u32[]{:S(2)}) collective-permute-start(bf16[128,3072]{1,0:T(8,128)(2,1)S(1)} %get-tuple-element.102), channel_id=1, source_target_pairs={{0,1},{1,0},{2,3},{3,2},{4,5},{5,4},{6,7},{7,6},{8,9},{9,8},{10,11... | collective-permute-start | bytes 2359304 | tf_op jit(solution)/shard_map/ppermute | solution.py:221
  137.8 18.0 %collective-permute-start.33 = (bf16[128,3072]{1,0:T(8,128)(2,1)S(1)}, bf16[128,3072]{1,0:T(8,128)(2,1)S(1)}, u32[]{:S(2)}, u32[]{:S(2)}) collective-permute-start(bf16[128,3072]{1,0:T(8,128)(2,1)S(1)} %get-tuple-element.97), channel_id=1, source_target_pairs={{0,1},{1,0},{2,3},{3,2},{4,5},{5,4},{6,7},{7,6},{8,9},{9,8},{10,11... | collective-permute-start | bytes 2359304 | tf_op jit(solution)/shard_map/ppermute | solution.py:221
  155.7 18.0 %collective-permute-start.35 = (bf16[128,3072]{1,0:T(8,128)(2,1)S(1)}, bf16[128,3072]{1,0:T(8,128)(2,1)S(1)}, u32[]{:S(2)}, u32[]{:S(2)}) collective-permute-start(bf16[128,3072]{1,0:T(8,128)(2,1)S(1)} %get-tuple-element.92), channel_id=1, source_target_pairs={{0,1},{1,0},{2,3},{3,2},{4,5},{5,4},{6,7},{7,6},{8,9},{9,8},{10,11... | collective-permute-start | bytes 2359304 | tf_op jit(solution)/shard_map/ppermute | solution.py:221
  173.7 9.4 %collective-permute-start.49 = (bf16[64,3072]{1,0:T(8,128)(2,1)S(1)}, bf16[64,3072]{1,0:T(8,128)(2,1)S(1)}, u32[]{:S(2)}, u32[]{:S(2)}) collective-permute-start(bf16[64,3072]{1,0:T(8,128)(2,1)S(1)} %add_convert_fusion.6), channel_id=1, source_target_pairs={{0,30},{1,3},{2,0},{3,5},{4,2},{5,7},{6,4},{7,9},{8,6},{9,11},{10,... | collective-permute-start | bytes 1179656 | tf_op jit(solution)/shard_map/ppermute | solution.py:221
  179.0 9.1 %collective-permute-start.36 = (bf16[64,3072]{1,0:T(8,128)(2,1)S(1)}, bf16[64,3072]{1,0:T(8,128)(2,1)S(1)}, u32[]{:S(2)}, u32[]{:S(2)}) collective-permute-start(bf16[64,3072]{1,0:T(8,128)(2,1)S(1)} %add_convert_fusion.12), channel_id=1, source_target_pairs={{0,30},{1,3},{2,0},{3,5},{4,2},{5,7},{6,4},{7,9},{8,6},{9,11},{10,... | collective-permute-start | bytes 1179656 | tf_op jit(solution)/shard_map/ppermute | solution.py:221
  183.2 9.1 %collective-permute-start.50 = (bf16[64,3072]{1,0:T(8,128)(2,1)S(1)}, bf16[64,3072]{1,0:T(8,128)(2,1)S(1)}, u32[]{:S(2)}, u32[]{:S(2)}) collective-permute-start(bf16[64,3072]{1,0:T(8,128)(2,1)S(1)} %add_convert_fusion.5), channel_id=1, source_target_pairs={{0,30},{1,3},{2,0},{3,5},{4,2},{5,7},{6,4},{7,9},{8,6},{9,11},{10,... | collective-permute-start | bytes 1179656 | tf_op jit(solution)/shard_map/ppermute | solution.py:221
  188.2 9.1 %collective-permute-start.38 = (bf16[64,3072]{1,0:T(8,128)(2,1)S(1)}, bf16[64,3072]{1,0:T(8,128)(2,1)S(1)}, u32[]{:S(2)}, u32[]{:S(2)}) collective-permute-start(bf16[64,3072]{1,0:T(8,128)(2,1)S(1)} %add_convert_fusion.11), channel_id=1, source_target_pairs={{0,30},{1,3},{2,0},{3,5},{4,2},{5,7},{6,4},{7,9},{8,6},{9,11},{10,... | collective-permute-start | bytes 1179656 | tf_op jit(solution)/shard_map/ppermute | solution.py:221
  192.5 9.1 %collective-permute-start.51 = (bf16[64,3072]{1,0:T(8,128)(2,1)S(1)}, bf16[64,3072]{1,0:T(8,128)(2,1)S(1)}, u32[]{:S(2)}, u32[]{:S(2)}) collective-permute-start(bf16[64,3072]{1,0:T(8,128)(2,1)S(1)} %add_convert_fusion.4), channel_id=1, source_target_pairs={{0,30},{1,3},{2,0},{3,5},{4,2},{5,7},{6,4},{7,9},{8,6},{9,11},{10,... | collective-permute-start | bytes 1179656 | tf_op jit(solution)/shard_map/ppermute | solution.py:221
  197.5 9.1 %collective-permute-start.53 = (bf16[64,3072]{1,0:T(8,128)(2,1)S(1)}, bf16[64,3072]{1,0:T(8,128)(2,1)S(1)}, u32[]{:S(2)}, u32[]{:S(2)}) collective-permute-start(bf16[64,3072]{1,0:T(8,128)(2,1)S(1)} %add_convert_fusion.10), channel_id=1, source_target_pairs={{0,30},{1,3},{2,0},{3,5},{4,2},{5,7},{6,4},{7,9},{8,6},{9,11},{10,... | collective-permute-start | bytes 1179656 | tf_op jit(solution)/shard_map/ppermute | solution.py:221
  202.5 9.6 %collective-permute-start.52 = (bf16[64,3072]{1,0:T(8,128)(2,1)}, bf16[64,3072]{1,0:T(8,128)(2,1)}, u32[]{:S(2)}, u32[]{:S(2)}) collective-permute-start(bf16[64,3072]{1,0:T(8,128)(2,1)} %add_convert_fusion.3), channel_id=1, source_target_pairs={{0,30},{1,3},{2,0},{3,5},{4,2},{5,7},{6,4},{7,9},{8,6},{9,11},{10,... | collective-permute-start | bytes 1179656 | tf_op jit(solution)/shard_map/ppermute | solution.py:221
  207.5 11.3 %collective-permute-start.56 = (bf16[64,3072]{1,0:T(8,128)(2,1)}, bf16[64,3072]{1,0:T(8,128)(2,1)}, u32[]{:S(2)}, u32[]{:S(2)}) collective-permute-start(bf16[64,3072]{1,0:T(8,128)(2,1)} %add_convert_fusion.2), channel_id=1, source_target_pairs={{0,30},{1,3},{2,0},{3,5},{4,2},{5,7},{6,4},{7,9},{8,6},{9,11},{10,... | collective-permute-start | bytes 1179656 | tf_op jit(solution)/shard_map/ppermute | solution.py:221
  (33 other events, 374.7 us)
